TPU v7x, 128 devices: a whole 4x4x4 slice. The times are simulated.
128 devices in a mesh: dp: 16 (over x, z), expert: 8 (over y, core).
Axes of the slice: x: 4, y: 4, z: 4, core: 2. Of those that a mesh axis runs over, the one named last changes fastest.
Arguments:
- tokens: bfloat16 [16384, 2048], P(('dp', 'expert')), may hold values from -6 to 6
- out_grad: bfloat16 [16384, 2048], P(('dp', 'expert')), may hold values from -3 to 3
- z_weight: float32 [16384], P(('dp', 'expert')), may hold values from 0.1 to 1
- router_weight: bfloat16 [2048, 128], replicated, may hold values from -0.125 to 0.125
- expert_ids: int32 [16384, 4], P(('dp', 'expert')), may hold values from 0 to 127, as said below
- gate_up_weight: bfloat16 [8, 2048, 3072], P('expert'), may hold values from -0.125 to 0.125
- down_weight: bfloat16 [8, 1536, 2048], P('expert'), may hold values from -0.15625 to 0.15625
Outputs:
- token_grad: bfloat16 [16384, 2048], P(('dp', 'expert'))
- router_grad: float32 [2048, 128], replicated
- gate_up_grad: bfloat16 [8, 2048, 3072], P('expert', 'dp')
- down_grad: bfloat16 [8, 1536, 2048], P('expert', 'dp')
Inputs may be any that keep to these rules, and one draw needn't show every extreme that they name: `expert_ids`: each row names 4 different experts. Experts 0 to 7 are the ones in flight. The 128 rows of one device name any one expert in flight at most 64 times; in every data group some expert in flight is named exactly 64 times by the rows of each device of the group.
All inputs are finite; a program needn't handle non-finite values.
Results may differ from a plain program's by a relative error of at most 0.019.
Values may be sent and summed in bfloat16 or wider, within the bound.
No kernel may reach another device: no remote copies, remote signals or barrier semaphores. Data moves between devices by JAX's collectives and lax.ppermute only.
A program may use at most 192 MiB of HBM per device.

v0:
```python
import functools

import jax
import jax.numpy as jnp
from jax import lax
from jax.experimental import pallas as pl
from jax.experimental.pallas import tpu as pltpu
from jax.sharding import Mesh, PartitionSpec as P


BF = jnp.bfloat16
F32 = jnp.float32
DP = ("x", "z")
GROUP = ("y", "c")


def shift(a, step):
    return lax.ppermute(a, "y", [(i, (i + step) % 4) for i in range(4)])


def swap(a):
    return lax.ppermute(a, "c", [(0, 1), (1, 0)])


def spread(left, right):
    half = left.shape[0] // 2
    return jnp.concatenate([shift(left[:half], 1), shift(right[half:], -1)], axis=0)


def tdot(a, b):
    return lax.dot_general(a, b, (((0,), (0,)), ((), ())), preferred_element_type=F32)


def dot_t(a, b):
    return lax.dot_general(a, b, (((1,), (1,)), ((), ())), preferred_element_type=F32)


def send_each(a):
    return lax.all_to_all(a, GROUP, split_axis=0, concat_axis=0, tiled=True)


def ring_all(a, axis):
    others = [lax.ppermute(a, axis, [(i, (i + k) % 4) for i in range(4)]) for k in (1, 2, 3)]
    return a + others[0] + others[1] + others[2]


LANES = 128


def grad_kernel(tiles, gate_a, gate_b, up_a, up_b, w_ref, xa_ref, xb_ref, dy_ref, prob_ref,
                parts_ref, pre_ref, score_ref, hid, dyk, x):
    i = pl.program_id(0)
    ff = hid.shape[1]
    tile = gate_a.shape[1]
    split = xa_ref.shape[0]

    @pl.when(i == 0)
    def _():
        score_ref[...] = jnp.zeros_like(score_ref)
        dyk[...] = (prob_ref[...] * dy_ref[...].astype(F32)).astype(BF)
        x[:split, :] = xa_ref[...]
        x[split:, :] = xb_ref[...]

    @pl.when(i < tiles)
    def _():
        at = pl.multiple_of(i * tile, tile)
        raw = lax.dot_general(dy_ref[...], w_ref[...], (((1,), (1,)), ((), ())), preferred_element_type=F32)
        gate = jnp.concatenate([gate_a[...], gate_b[...]], axis=0)
        up = jnp.concatenate([up_a[...], up_b[...]], axis=0)
        sig = 1.0 / (1.0 + jnp.exp(-gate))
        silu = gate * sig
        hidden = (silu * up).astype(BF)
        score_ref[...] += jnp.sum(hidden.astype(F32) * raw, axis=1, keepdims=True)
        grad = prob_ref[...] * raw
        hid[:, pl.ds(at, tile)] = hidden
        pre_ref[:, pl.ds(at, tile)] = (grad * up * sig * (1.0 + gate * (1.0 - sig))).astype(BF)
        pre_ref[:, pl.ds(pl.multiple_of(ff + at, tile), tile)] = (grad * silu).astype(BF)

    def emit(left, right, base, r):
        cols = 512 if right.shape[1] % 512 == 0 else right.shape[1]
        for q in range(right.shape[1] // cols):
            g = jnp.dot(left, right[:, q * cols : (q + 1) * cols], preferred_element_type=F32).astype(BF)
            for t in range(cols // LANES):
                at = base + (q * (cols // LANES) + t) * r
                for d in range(4):
                    parts_ref[d, at : at + r, :] = g[d * r : (d + 1) * r, t * LANES : (t + 1) * LANES]

    @pl.when(i >= tiles)
    def _():
        k = i - tiles
        r = x.shape[1] // 16
        emit(x[:, pl.ds(pl.multiple_of(k * 4 * r, 4 * r), 4 * r)].T, pre_ref, 0, r)
        base = 2 * ff // LANES * r
        r = ff // 16
        emit(hid[:, pl.ds(pl.multiple_of(k * 4 * r, 4 * r), 4 * r)].T, dyk, base, r)


def weight_grads(act_a, act_b, w_dn, xa, xb, dy, row_prob):
    rows, width = dy.shape
    ff = w_dn.shape[0]
    tiles = 6
    tile = ff // tiles
    depth = (2 * ff * (width // 16) + width * (ff // 16)) // LANES
    na, nb = xa.shape[0], xb.shape[0]
    last = tiles - 1
    whole = lambda i: (0, 0)
    low = lambda i: (0, jnp.minimum(i, last))
    high = lambda i: (0, tiles + jnp.minimum(i, last))
    return pl.pallas_call(
        functools.partial(grad_kernel, tiles),
        grid=(tiles + 4,),
        in_specs=[
            pl.BlockSpec((na, tile), low),
            pl.BlockSpec((nb, tile), low),
            pl.BlockSpec((na, tile), high),
            pl.BlockSpec((nb, tile), high),
            pl.BlockSpec((tile, width), lambda i: (jnp.minimum(i, last), 0)),
            pl.BlockSpec((na, width), whole),
            pl.BlockSpec((nb, width), whole),
            pl.BlockSpec((rows, width), whole),
            pl.BlockSpec((rows, 1), whole),
        ],
        out_specs=[
            pl.BlockSpec((4, depth, LANES), lambda i: (jnp.maximum(i - tiles, 0), 0, 0)),
            pl.BlockSpec((rows, 2 * ff), whole),
            pl.BlockSpec((rows, 1), whole),
        ],
        out_shape=[
            jax.ShapeDtypeStruct((16, depth, LANES), BF),
            pltpu.HBM((rows, 2 * ff), BF),
            jax.ShapeDtypeStruct((rows, 1), F32),
        ],
        scratch_shapes=[
            pltpu.VMEM((rows, ff), BF),
            pltpu.VMEM((rows, width), BF),
            pltpu.VMEM((rows, width), BF),
        ],
        compiler_params=pltpu.CompilerParams(vmem_limit_bytes=36 * 2**20),
        cost_estimate=pl.CostEstimate(
            flops=2 * rows * width * ff * 4, bytes_accessed=36 * 2**20, transcendentals=rows * ff
        ),
        name="weight_grads",
    )(act_a, act_b, act_a, act_b, w_dn, xa, xb, dy, row_prob)


def unpack_kernel(in_ref, gu_ref, dn_ref):
    at = 0
    for ref in (gu_ref, dn_ref):
        r = ref.shape[0]
        for t in range(ref.shape[1] // LANES):
            ref[:, t * LANES : (t + 1) * LANES] = in_ref[at : at + r, :]
            at += r


def unpack(total, width, ff):
    return pl.pallas_call(
        unpack_kernel,
        out_shape=[
            jax.ShapeDtypeStruct((width // 16, 2 * ff), BF),
            jax.ShapeDtypeStruct((ff // 16, width), BF),
        ],
        name="unpack",
    )(total)


def step(tokens, out_grad, z_weight, router_weight, expert_ids, gate_up_weight, down_weight):
    tok, width = tokens.shape
    routed = router_weight.shape[1]
    cap = tok // 2
    w_gu = gate_up_weight[0]
    w_dn = down_weight[0]
    ff = w_dn.shape[0]
    my_y = lax.axis_index("y")
    my_c = lax.axis_index("c")

    names = jnp.arange(routed, dtype=jnp.int32)[None, :]
    slots = jnp.arange(cap, dtype=F32)[None, :, None]
    before = (jnp.arange(tok)[:, None] < jnp.arange(tok)[None, :]).astype(BF)
    top = expert_ids.shape[1]
    id_row = expert_ids.T.astype(BF).reshape(1, top * tok)
    x0 = jnp.concatenate([tokens, jnp.pad(id_row, ((0, 7), (0, width - top * tok)))], axis=0)
    logits = jnp.dot(tokens, router_weight, preferred_element_type=F32)
    chosen = expert_ids[:, 0:1] == names
    for k in range(1, top):
        chosen = chosen | (expert_ids[:, k : k + 1] == names)
    expl = jnp.exp(logits)
    sel_exp = jnp.where(chosen, expl, 0.0)
    probs = jnp.where(chosen, sel_exp / jnp.sum(sel_exp, axis=1, keepdims=True), 0.0)
    log_total = jnp.log(jnp.sum(expl, axis=1, keepdims=True))
    mine = probs[:, :8].T
    high = mine.astype(BF)
    low = (mine - high.astype(F32)).astype(BF)
    prob_row = jnp.concatenate([high.reshape(1, 8 * tok), low.reshape(1, 8 * tok)], axis=1)
    g0 = jnp.concatenate([out_grad, jnp.pad(prob_row, ((0, 7), (0, width - 16 * tok)))], axis=0)

    x1, x3 = shift(x0, 1), shift(x0, -1)
    g1, g3 = shift(g0, 1), shift(g0, -1)
    x2 = spread(x1, x3)
    g2 = spread(g1, g3)
    x_parts, g_parts = [], []
    for part in (x0, x1, x3, x2):
        x_parts += [part, swap(part)]
    for part in (g0, g1, g3, g2):
        g_parts += [part, swap(part)]
    gray = lambda k: k ^ (k >> 1)
    place = [gray((my_y - s // 2) % 4) * 2 + (my_c ^ (s % 2)) for s in range(8)]
    origin = [((my_y - gray(k)) % 4) * 2 + (my_c ^ cc) for k in range(4) for cc in range(2)]

    me = my_y * 2 + my_c

    def choose(parts):
        named = jnp.stack([p[tok, : top * tok].reshape(top, tok) for p in parts])
        member = jnp.max(jnp.where(named == me.astype(BF), 1.0, 0.0), axis=1)
        rank = jnp.dot(member.astype(BF), before, preferred_element_type=F32)
        return (rank[:, None, :] == slots) & (member[:, None, :] > 0.0)

    def compact(take, parts):
        rows = [
            jnp.dot(take[j].astype(BF), p[:tok], preferred_element_type=F32).astype(BF)
            for j, p in enumerate(parts)
        ]
        return jnp.concatenate(rows, axis=0)

    take_a = choose(x_parts[:6])
    xa = compact(take_a, x_parts[:6])
    act_a = jnp.dot(xa, w_gu, preferred_element_type=F32)
    take_b = choose(x_parts[6:])
    xb = compact(take_b, x_parts[6:])
    act_b = jnp.dot(xb, w_gu, preferred_element_type=F32)
    take = jnp.concatenate([take_a, take_b], axis=0)
    pick = (jnp.arange(16, dtype=jnp.int32) % 8 == me)[None, :, None]
    pairs = jnp.stack([p[tok, : 16 * tok].reshape(16, tok) for p in g_parts]).astype(F32)
    prob_of = jnp.sum(jnp.where(pick, pairs, 0.0), axis=1)
    row_prob = jnp.sum(jnp.where(take, prob_of[:, None, :], 0.0), axis=2).reshape(8 * cap, 1)
    dy = compact(take, g_parts)
    parts, pre, score = weight_grads(act_a, act_b, w_dn, xa, xb, dy, row_prob)
    total = lax.psum_scatter(parts.reshape(1, -1, parts.shape[2]), DP, scatter_dimension=1, tiled=True)[0]
    gate_up_grad, down_grad = unpack(total, width, ff)

    home_score = send_each(jnp.concatenate(
        [lax.dynamic_slice_in_dim(score.reshape(8, 1, cap), s, 1, 0) for s in place], axis=0))
    row_grad = dot_t(pre, w_gu).astype(BF)
    row_grad = row_grad.reshape(8, cap, width)
    home_rows = send_each(jnp.concatenate(
        [lax.dynamic_slice_in_dim(row_grad, s, 1, 0) for s in place], axis=0))

    member = jnp.where(chosen[:, :8], 1.0, 0.0).T
    rank = jnp.dot(member.astype(BF), before, preferred_element_type=F32)
    back = (rank[:, None, :] == slots) & (member[:, None, :] > 0.0)
    score_of = jnp.sum(jnp.where(back, home_score.reshape(8, cap, 1), 0.0), axis=1)
    scores = jnp.concatenate([score_of.T, jnp.zeros((tok, routed - 8), F32)], axis=1)
    mean_score = jnp.sum(probs * scores, axis=1, keepdims=True)
    z_grad = 2.0 * z_weight[:, None] * log_total * jnp.exp(logits - log_total)
    logit_grad = (z_grad + probs * (scores - mean_score)).astype(BF)
    share = send_each(logit_grad.T.reshape(8, routed // 8, tok))
    share = jnp.concatenate([lax.dynamic_slice_in_dim(share, o, 1, 0)[0] for o in origin], axis=1)
    group_tokens = jnp.concatenate([p[:tok] for p in x_parts], axis=0)
    router_part = jnp.dot(share, group_tokens, preferred_element_type=F32)
    router_part = ring_all(ring_all(router_part, "x"), "z")
    near = lax.all_gather(router_part, "y", axis=0, tiled=False)
    away = swap(near)
    both = jnp.stack([jnp.where(my_c == 0, near, away), jnp.where(my_c == 0, away, near)], axis=1)
    router_grad = both.reshape(routed, width).T
    token_grad = (
        tdot(back.astype(BF).reshape(8 * cap, tok), home_rows.reshape(8 * cap, width))
        + dot_t(logit_grad, router_weight)
    ).astype(BF)
    return token_grad, router_grad, gate_up_grad[None], down_grad[None]


def solution(mesh):
    grid = Mesh(mesh.devices.reshape(4, 4, 4, 2), ("x", "z", "y", "c"))
    every = ("x", "z", "y", "c")
    return jax.shard_map(
        step,
        mesh=grid,
        in_specs=(
            P(every, None),
            P(every, None),
            P(every),
            P(),
            P(every, None),
            P(GROUP, None, None),
            P(GROUP, None, None),
        ),
        out_specs=(
            P(every, None),
            P(),
            P(GROUP, DP, None),
            P(GROUP, DP, None),
        ),
        check_vma=False,
    )
```

profile of v0, /device:TPU:0, one launch (start us, length us, event | category | flops | bytes accessed | tf_op | source)
XLA Modules:
  0.0 249.2 jit_solution(9365456717420541077)
XLA Ops:
  17.8 11.2 %collective-permute-done.11 = bf16[136,2048]{1,0:T(8,128)(2,1)S(1)} collective-permute-done((bf16[136,2048]{1,0:T(8,128)(2,1)}, bf16[136,2048]{1,0:T(8,128)(2,1)S(1)}, u32[]{:S(2)}, u32[]{:S(2)}) %collective-permute-start.11) | collective-permute-done | bytes 557088 | tf_op jit(solution)/shard_map/ppermute | solution.py:18
  29.2 2.8 %collective-permute-start.14 = (bf16[68,2048]{1,0:T(8,128)(2,1)S(1)}, bf16[68,2048]{1,0:T(8,128)(2,1)S(1)}, u32[]{:S(2)}, u32[]{:S(2)}) collective-permute-start(bf16[68,2048]{1,0:T(8,128)(2,1)S(1)} %slice.234), channel_id=1, source_target_pairs={{0,6},{2,0},{4,2},{6,4},{1,7},{3,1},{5,3},{7,5},{8,14},{10,8},{12,... | collective-permute-start | bytes 835592 | tf_op jit(solution)/shard_map/ppermute | solution.py:18
  33.0 8.0 %collective-permute-done.3 = bf16[136,2048]{1,0:T(8,128)(2,1)S(1)} collective-permute-done((bf16[136,2048]{1,0:T(8,128)(2,1)}, bf16[136,2048]{1,0:T(8,128)(2,1)S(1)}, u32[]{:S(2)}, u32[]{:S(2)}) %collective-permute-start.3) | collective-permute-done | bytes 557088 | tf_op jit(solution)/shard_map/ppermute | solution.py:18
  47.4 4.9 %collective-permute-done.5 = bf16[68,2048]{1,0:T(8,128)(2,1)S(1)} collective-permute-done((bf16[68,2048]{1,0:T(8,128)(2,1)S(1)}, bf16[68,2048]{1,0:T(8,128)(2,1)S(1)}, u32[]{:S(2)}, u32[]{:S(2)}) %collective-permute-start.5) | collective-permute-done | bytes 278560 | tf_op jit(solution)/shard_map/ppermute | solution.py:18
  52.3 2.6 %collective-permute-done.6 = bf16[68,2048]{1,0:T(8,128)(2,1)S(1)} collective-permute-done((bf16[68,2048]{1,0:T(8,128)(2,1)S(1)}, bf16[68,2048]{1,0:T(8,128)(2,1)S(1)}, u32[]{:S(2)}, u32[]{:S(2)}) %collective-permute-start.6) | collective-permute-done | bytes 278560 | tf_op jit(solution)/shard_map/ppermute | solution.py:18
  58.2 11.7 %fusion.4.gate_a.up_a = f32[384,3072]{1,0:T(8,128)} fusion(bf16[384,2048]{1,0:T(8,128)(2,1)S(1)} %fusion.18.xa_ref, bf16[1,2048,3072]{2,1,0:T(8,128)(2,1)} %param.12), kind=kOutput, calls=%fused_computation.4 | convolution fusion | flops 4831838208 | bytes 18874368 | tf_op jit(solution)/shard_map/dot_general | solution.py:226
  81.6 2.8 %copy-done.5 = bf16[1,1536,2048]{2,1,0:T(8,128)(2,1)S(1)} copy-done((bf16[1,1536,2048]{2,1,0:T(8,128)(2,1)S(1)}, bf16[1,1536,2048]{2,1,0:T(8,128)(2,1)}, u32[]{:S(2)}) %copy-start.5) | copy-done | bytes 6291480
  84.4 2.3 copy-done.6
  86.8 21.4 %weight_grads.1 = (bf16[16,4608,128]{2,1,0:T(8,128)(2,1)}, bf16[512,3072]{1,0:T(8,128)(2,1)}, f32[512,1]{1,0:T(8,128)S(1)}) custom-call(f32[384,3072]{1,0:T(8,128)S(1)} %copy-done.6, f32[128,3072]{1,0:T(8,128)S(1)} %fusion.2.gate_b.up_b, f32[384,3072]{1,0:T(8,128)S(1)} %copy-done.6, f32[128,3072]{1,0:T(8,128)S(1)} %fusion.2.gate_b.up_b, ...), custom_call_target="tpu_custom_call" | custom-call | flops 12884901888 | bytes 37748736 | tf_op jit(solution)/shard_map/weight_grads/pallas_call | solution.py:109
  116.0 3.5 %all-to-all-start.1 = ((f32[8,1,64]{2,1,0:T(1,128)}), f32[8,1,64]{2,1,0:T(1,128)S(1)}, u32[]{:S(2)}, u32[]{:S(2)}) async-start(f32[8,1,64]{2,1,0:T(1,128)} %bitcast.22), calls=%async_computation.1 | async-start | bytes 8192 | tf_op jit(solution)/shard_map/all_to_all | solution.py:39
  119.5 10.7 %fusion.6 = bf16[512,2048]{1,0:T(8,128)(2,1)S(1)} fusion(bf16[512,3072]{1,0:T(8,128)(2,1)} %get-tuple-element.9, bf16[1,2048,3072]{2,1,0:T(8,128)(2,1)} %param.12), kind=kOutput, calls=%fused_computation.6 | convolution fusion | flops 6443499520 | bytes 17825792 | tf_op jit(solution)/shard_map/dot_general | solution.py:35
  135.5 4.5 %all-to-all-start.2 = ((bf16[8,16,128]{2,1,0:T(8,128)(2,1)}), bf16[8,16,128]{2,1,0:T(8,128)(2,1)S(1)}, u32[]{:S(2)}, u32[]{:S(2)}) async-start(bf16[8,16,128]{2,1,0:T(8,128)(2,1)} %bitcast.26), calls=%async_computation.2 | async-start | bytes 65536 | tf_op jit(solution)/shard_map/all_to_all | solution.py:39
  140.7 4.7 %all-to-all-done.2 = bf16[8,16,128]{2,1,0:T(8,128)(2,1)S(1)} async-done(((bf16[8,16,128]{2,1,0:T(8,128)(2,1)}), bf16[8,16,128]{2,1,0:T(8,128)(2,1)S(1)}, u32[]{:S(2)}, u32[]{:S(2)}) %all-to-all-start.2) | async-done | bytes 32800 | tf_op jit(solution)/shard_map/all_to_all | solution.py:39
  145.6 2.9 %fusion.84 = f32[16,2048]{1,0:T(8,128)S(1)} fusion(bf16[16,1024]{1,0:T(8,128)(2,1)S(1)} %constant_dynamic-update-slice_fusion.14, bf16[1024,2048]{1,0:T(8,128)(2,1)} %slice_dynamic-update-slice_fusion), kind=kOutput, calls=%fused_computation.222 | convolution fusion | flops 67108864 | bytes 4358144 | tf_op jit(solution)/shard_map/dot_general | solution.py:258
  149.9 2.7 %collective-permute-start.17 = (f32[16,2048]{1,0:T(8,128)S(1)}, f32[16,2048]{1,0:T(8,128)S(1)}, u32[]{:S(2)}, u32[]{:S(2)}) collective-permute-start(f32[16,2048]{1,0:T(8,128)S(1)} %fusion.84), channel_id=1, source_target_pairs={{0,64},{32,96},{64,0},{96,32},{1,65},{33,97},{65,1},{97,33},{2,66}... | collective-permute-start | bytes 393224 | tf_op jit(solution)/shard_map/ppermute | solution.py:43
  154.8 3.9 %collective-permute-done.16 = f32[16,2048]{1,0:T(8,128)S(1)} collective-permute-done((f32[16,2048]{1,0:T(8,128)S(1)}, f32[16,2048]{1,0:T(8,128)S(1)}, u32[]{:S(2)}, u32[]{:S(2)}) %collective-permute-start.16) | collective-permute-done | bytes 131104 | tf_op jit(solution)/shard_map/ppermute | solution.py:43
  158.7 6.3 %collective-permute-done.17 = f32[16,2048]{1,0:T(8,128)S(1)} collective-permute-done((f32[16,2048]{1,0:T(8,128)S(1)}, f32[16,2048]{1,0:T(8,128)S(1)}, u32[]{:S(2)}, u32[]{:S(2)}) %collective-permute-start.17) | collective-permute-done | bytes 131104 | tf_op jit(solution)/shard_map/ppermute | solution.py:43
  167.0 3.7 %collective-permute-start.20 = (f32[16,2048]{1,0:T(8,128)S(1)}, f32[16,2048]{1,0:T(8,128)S(1)}, u32[]{:S(2)}, u32[]{:S(2)}) collective-permute-start(f32[16,2048]{1,0:T(8,128)S(1)} %add_add_fusion.1), channel_id=1, source_target_pairs={{0,16},{8,24},{16,0},{24,8},{1,17},{9,25},{17,1},{25,9},{2,18},{10... | collective-permute-start | bytes 393224 | tf_op jit(solution)/shard_map/ppermute | solution.py:43
  172.5 3.6 %all-to-all-start = ((bf16[8,64,2048]{2,1,0:T(8,128)(2,1)}), bf16[8,64,2048]{2,1,0:T(8,128)(2,1)S(1)}, u32[]{:S(2)}, u32[]{:S(2)}) async-start(bf16[8,64,2048]{2,1,0:T(8,128)(2,1)} %dynamic-slice_dynamic-update-slice_fusion), calls=%async_computation | async-start | bytes 4194304 | tf_op jit(solution)/shard_map/all_to_all | solution.py:39
  176.1 6.6 %collective-permute-done.20 = f32[16,2048]{1,0:T(8,128)S(1)} collective-permute-done((f32[16,2048]{1,0:T(8,128)S(1)}, f32[16,2048]{1,0:T(8,128)S(1)}, u32[]{:S(2)}, u32[]{:S(2)}) %collective-permute-start.20) | collective-permute-done | bytes 131104 | tf_op jit(solution)/shard_map/ppermute | solution.py:43
  182.7 28.4 %all-gather = f32[64,2048]{1,0:T(8,128)S(1)} all-gather(f32[16,2048]{1,0:T(8,128)S(1)} %add_add_fusion), channel_id=2, replica_groups=mesh['x'=4,'z'=4,'y'=4,'c'=2] {'y'}, dimensions={0}, use_global_device_ids=true | all-gather | bytes 655360 | tf_op jit(solution)/shard_map/all_gather | solution.py:260
  215.4 2.8 %copy.18 = f32[2048,128]{1,0:T(8,128)} copy(f32[2048,128]{0,1:T(8,128)} %bitcast.188) | data formatting | bytes 2097152
  220.7 19.1 %reduce-scatter.2.cloned.1.call-done = bf16[1,4608,128]{2,1,0:T(8,128)(2,1)} async-done(((bf16[1,73728,128]{2,1,0:T(8,128)(2,1)}), bf16[1,4608,128]{2,1,0:T(8,128)(2,1)}) %reduce-scatter.2.cloned.1.call-update) | async-done | bytes 1179664 | tf_op jit(solution)/shard_map/reduce_scatter | solution.py:237
  239.8 2.6 %unpack.1 = (bf16[128,3072]{1,0:T(8,128)(2,1)}, bf16[96,2048]{1,0:T(8,128)(2,1)}) custom-call(bf16[4608,128]{1,0:T(8,128)(2,1)} %bitcast.199), custom_call_target="tpu_custom_call" | custom-call | tf_op jit(solution)/shard_map/unpack/pallas_call | solution.py:156
  (225 shorter events, 60.4 us)
Async XLA Ops:
  7.2 232.6 %reduce-scatter.2.cloned.1.call-start = ((), (), s32[]{:S(2)}) async-start(), calls=%async_computation.4 | async-start | bytes 20054016 | tf_op jit(solution)/shard_map/reduce_scatter | solution.py:237
  11.7 17.5 %collective-permute-start.9 = (bf16[136,2048]{1,0:T(8,128)(2,1)}, bf16[136,2048]{1,0:T(8,128)(2,1)}, u32[]{:S(2)}, u32[]{:S(2)}) collective-permute-start(bf16[136,2048]{1,0:T(8,128)(2,1)} %pad_maximum_fusion.3), channel_id=1, source_target_pairs={{0,2},{2,4},{4,6},{6,0},{1,3},{3,5},{5,7},{7,1},{8,10},{10,12},{12... | collective-permute-start | bytes 1671176 | tf_op jit(solution)/shard_map/ppermute | solution.py:18
  13.4 15.7 %collective-permute-start.11 = (bf16[136,2048]{1,0:T(8,128)(2,1)}, bf16[136,2048]{1,0:T(8,128)(2,1)S(1)}, u32[]{:S(2)}, u32[]{:S(2)}) collective-permute-start(bf16[136,2048]{1,0:T(8,128)(2,1)} %pad_maximum_fusion.3), channel_id=1, source_target_pairs={{0,6},{2,0},{4,2},{6,4},{1,7},{3,1},{5,3},{7,5},{8,14},{10,8},{12,... | collective-permute-start | bytes 1671176 | tf_op jit(solution)/shard_map/ppermute | solution.py:18
  15.8 25.2 %collective-permute-start.3 = (bf16[136,2048]{1,0:T(8,128)(2,1)}, bf16[136,2048]{1,0:T(8,128)(2,1)S(1)}, u32[]{:S(2)}, u32[]{:S(2)}) collective-permute-start(bf16[136,2048]{1,0:T(8,128)(2,1)} %fusion.25), channel_id=1, source_target_pairs={{0,6},{2,0},{4,2},{6,4},{1,7},{3,1},{5,3},{7,5},{8,14},{10,8},{12,... | collective-permute-start | bytes 1671176 | tf_op jit(solution)/shard_map/ppermute | solution.py:18
  17.7 25.0 %collective-permute-start.1 = (bf16[136,2048]{1,0:T(8,128)(2,1)}, bf16[136,2048]{1,0:T(8,128)(2,1)S(1)}, u32[]{:S(2)}, u32[]{:S(2)}) collective-permute-start(bf16[136,2048]{1,0:T(8,128)(2,1)} %fusion.25), channel_id=1, source_target_pairs={{0,2},{2,4},{4,6},{6,0},{1,3},{3,5},{5,7},{7,1},{8,10},{10,12},{12... | collective-permute-start | bytes 1671176 | tf_op jit(solution)/shard_map/ppermute | solution.py:18
  17.8 26.6 %collective-permute-start = (bf16[136,2048]{1,0:T(8,128)(2,1)}, bf16[136,2048]{1,0:T(8,128)(2,1)S(1)}, u32[]{:S(2)}, u32[]{:S(2)}) collective-permute-start(bf16[136,2048]{1,0:T(8,128)(2,1)} %fusion.25), channel_id=1, source_target_pairs={{0,1},{1,0},{2,3},{3,2},{4,5},{5,4},{6,7},{7,6},{8,9},{9,8},{10,11... | collective-permute-start | bytes 1671176 | tf_op jit(solution)/shard_map/ppermute | solution.py:22
  29.1 15.9 %collective-permute-start.8 = (bf16[136,2048]{1,0:T(8,128)(2,1)}, bf16[136,2048]{1,0:T(8,128)(2,1)S(1)}, u32[]{:S(2)}, u32[]{:S(2)}) collective-permute-start(bf16[136,2048]{1,0:T(8,128)(2,1)} %pad_maximum_fusion.3), channel_id=1, source_target_pairs={{0,1},{1,0},{2,3},{3,2},{4,5},{5,4},{6,7},{7,6},{8,9},{9,8},{10,11... | collective-permute-start | bytes 1671176 | tf_op jit(solution)/shard_map/ppermute | solution.py:22
  29.2 18.1 %collective-permute-start.14 = (bf16[68,2048]{1,0:T(8,128)(2,1)S(1)}, bf16[68,2048]{1,0:T(8,128)(2,1)S(1)}, u32[]{:S(2)}, u32[]{:S(2)}) collective-permute-start(bf16[68,2048]{1,0:T(8,128)(2,1)S(1)} %slice.234), channel_id=1, source_target_pairs={{0,6},{2,0},{4,2},{6,4},{1,7},{3,1},{5,3},{7,5},{8,14},{10,8},{12,... | collective-permute-start | bytes 835592 | tf_op jit(solution)/shard_map/ppermute | solution.py:18
  41.0 14.0 %collective-permute-start.13 = (bf16[68,2048]{1,0:T(8,128)(2,1)S(1)}, bf16[68,2048]{1,0:T(8,128)(2,1)S(1)}, u32[]{:S(2)}, u32[]{:S(2)}) collective-permute-start(bf16[68,2048]{1,0:T(8,128)(2,1)S(1)} %slice.233), channel_id=1, source_target_pairs={{0,2},{2,4},{4,6},{6,0},{1,3},{3,5},{5,7},{7,1},{8,10},{10,12},{12... | collective-permute-start | bytes 835592 | tf_op jit(solution)/shard_map/ppermute | solution.py:18
  42.7 9.5 %collective-permute-start.5 = (bf16[68,2048]{1,0:T(8,128)(2,1)S(1)}, bf16[68,2048]{1,0:T(8,128)(2,1)S(1)}, u32[]{:S(2)}, u32[]{:S(2)}) collective-permute-start(bf16[68,2048]{1,0:T(8,128)(2,1)S(1)} %slice.218), channel_id=1, source_target_pairs={{0,6},{2,0},{4,2},{6,4},{1,7},{3,1},{5,3},{7,5},{8,14},{10,8},{12,... | collective-permute-start | bytes 835592 | tf_op jit(solution)/shard_map/ppermute | solution.py:18
  44.5 10.4 %collective-permute-start.6 = (bf16[68,2048]{1,0:T(8,128)(2,1)S(1)}, bf16[68,2048]{1,0:T(8,128)(2,1)S(1)}, u32[]{:S(2)}, u32[]{:S(2)}) collective-permute-start(bf16[68,2048]{1,0:T(8,128)(2,1)S(1)} %slice.220), channel_id=1, source_target_pairs={{0,2},{2,4},{4,6},{6,0},{1,3},{3,5},{5,7},{7,1},{8,10},{10,12},{12... | collective-permute-start | bytes 835592 | tf_op jit(solution)/shard_map/ppermute | solution.py:18
  45.8 9.9 %collective-permute-start.2 = (bf16[136,2048]{1,0:T(8,128)(2,1)S(1)}, bf16[136,2048]{1,0:T(8,128)(2,1)S(1)}, u32[]{:S(2)}, u32[]{:S(2)}) collective-permute-start(bf16[136,2048]{1,0:T(8,128)(2,1)S(1)} %collective-permute-done.1), channel_id=1, source_target_pairs={{0,1},{1,0},{2,3},{3,2},{4,5},{5,4},{6,7},{7,6},{8,9},{9,8},{10,11... | collective-permute-start | bytes 1671176 | tf_op jit(solution)/shard_map/ppermute | solution.py:22
  47.3 8.7 %collective-permute-start.4 = (bf16[136,2048]{1,0:T(8,128)(2,1)S(1)}, bf16[136,2048]{1,0:T(8,128)(2,1)S(1)}, u32[]{:S(2)}, u32[]{:S(2)}) collective-permute-start(bf16[136,2048]{1,0:T(8,128)(2,1)S(1)} %collective-permute-done.3), channel_id=1, source_target_pairs={{0,1},{1,0},{2,3},{3,2},{4,5},{5,4},{6,7},{7,6},{8,9},{9,8},{10,11... | collective-permute-start | bytes 1671176 | tf_op jit(solution)/shard_map/ppermute | solution.py:22
  55.0 17.1 %collective-permute-start.7 = (bf16[136,2048]{1,0:T(8,128)(2,1)S(1)}, bf16[136,2048]{1,0:T(8,128)(2,1)S(1)}, u32[]{:S(2)}, u32[]{:S(2)}) collective-permute-start(bf16[136,2048]{1,0:T(8,128)(2,1)S(1)} %pad_maximum_fusion.1), channel_id=1, source_target_pairs={{0,1},{1,0},{2,3},{3,2},{4,5},{5,4},{6,7},{7,6},{8,9},{9,8},{10,11... | collective-permute-start | bytes 1671176 | tf_op jit(solution)/shard_map/ppermute | solution.py:22
  55.7 19.1 %collective-permute-start.15 = (bf16[136,2048]{1,0:T(8,128)(2,1)S(1)}, bf16[136,2048]{1,0:T(8,128)(2,1)S(1)}, u32[]{:S(2)}, u32[]{:S(2)}) collective-permute-start(bf16[136,2048]{1,0:T(8,128)(2,1)S(1)} %pad_maximum_fusion.2), channel_id=1, source_target_pairs={{0,1},{1,0},{2,3},{3,2},{4,5},{5,4},{6,7},{7,6},{8,9},{9,8},{10,11... | collective-permute-start | bytes 1671176 | tf_op jit(solution)/shard_map/ppermute | solution.py:22
  116.0 18.7 %all-to-all-start.1 = ((f32[8,1,64]{2,1,0:T(1,128)}), f32[8,1,64]{2,1,0:T(1,128)S(1)}, u32[]{:S(2)}, u32[]{:S(2)}) async-start(f32[8,1,64]{2,1,0:T(1,128)} %bitcast.22), calls=%async_computation.1 | async-start | bytes 8192 | tf_op jit(solution)/shard_map/all_to_all | solution.py:39
  135.5 9.9 %all-to-all-start.2 = ((bf16[8,16,128]{2,1,0:T(8,128)(2,1)}), bf16[8,16,128]{2,1,0:T(8,128)(2,1)S(1)}, u32[]{:S(2)}, u32[]{:S(2)}) async-start(bf16[8,16,128]{2,1,0:T(8,128)(2,1)} %bitcast.26), calls=%async_computation.2 | async-start | bytes 65536 | tf_op jit(solution)/shard_map/all_to_all | solution.py:39
  148.5 10.2 %collective-permute-start.16 = (f32[16,2048]{1,0:T(8,128)S(1)}, f32[16,2048]{1,0:T(8,128)S(1)}, u32[]{:S(2)}, u32[]{:S(2)}) collective-permute-start(f32[16,2048]{1,0:T(8,128)S(1)} %fusion.84), channel_id=1, source_target_pairs={{0,32},{32,64},{64,96},{96,0},{1,33},{33,65},{65,97},{97,1},{2,34}... | collective-permute-start | bytes 393224 | tf_op jit(solution)/shard_map/ppermute | solution.py:43
  149.9 15.1 %collective-permute-start.17 = (f32[16,2048]{1,0:T(8,128)S(1)}, f32[16,2048]{1,0:T(8,128)S(1)}, u32[]{:S(2)}, u32[]{:S(2)}) collective-permute-start(f32[16,2048]{1,0:T(8,128)S(1)} %fusion.84), channel_id=1, source_target_pairs={{0,64},{32,96},{64,0},{96,32},{1,65},{33,97},{65,1},{97,33},{2,66}... | collective-permute-start | bytes 393224 | tf_op jit(solution)/shard_map/ppermute | solution.py:43
  152.6 12.4 %collective-permute-start.18 = (f32[16,2048]{1,0:T(8,128)S(1)}, f32[16,2048]{1,0:T(8,128)S(1)}, u32[]{:S(2)}, u32[]{:S(2)}) collective-permute-start(f32[16,2048]{1,0:T(8,128)S(1)} %fusion.84), channel_id=1, source_target_pairs={{0,96},{32,0},{64,32},{96,64},{1,97},{33,1},{65,33},{97,65},{2,98}... | collective-permute-start | bytes 393224 | tf_op jit(solution)/shard_map/ppermute | solution.py:43
  165.0 11.1 %collective-permute-start.19 = (f32[16,2048]{1,0:T(8,128)S(1)}, f32[16,2048]{1,0:T(8,128)S(1)}, u32[]{:S(2)}, u32[]{:S(2)}) collective-permute-start(f32[16,2048]{1,0:T(8,128)S(1)} %add_add_fusion.1), channel_id=1, source_target_pairs={{0,8},{8,16},{16,24},{24,0},{1,9},{9,17},{17,25},{25,1},{2,10},{10... | collective-permute-start | bytes 393224 | tf_op jit(solution)/shard_map/ppermute | solution.py:43
  167.0 15.7 %collective-permute-start.20 = (f32[16,2048]{1,0:T(8,128)S(1)}, f32[16,2048]{1,0:T(8,128)S(1)}, u32[]{:S(2)}, u32[]{:S(2)}) collective-permute-start(f32[16,2048]{1,0:T(8,128)S(1)} %add_add_fusion.1), channel_id=1, source_target_pairs={{0,16},{8,24},{16,0},{24,8},{1,17},{9,25},{17,1},{25,9},{2,18},{10... | collective-permute-start | bytes 393224 | tf_op jit(solution)/shard_map/ppermute | solution.py:43
  170.7 12.0 %collective-permute-start.21 = (f32[16,2048]{1,0:T(8,128)S(1)}, f32[16,2048]{1,0:T(8,128)S(1)}, u32[]{:S(2)}, u32[]{:S(2)}) collective-permute-start(f32[16,2048]{1,0:T(8,128)S(1)} %add_add_fusion.1), channel_id=1, source_target_pairs={{0,24},{8,0},{16,8},{24,16},{1,25},{9,1},{17,9},{25,17},{2,26},{10... | collective-permute-start | bytes 393224 | tf_op jit(solution)/shard_map/ppermute | solution.py:43
  172.5 45.8 %all-to-all-start = ((bf16[8,64,2048]{2,1,0:T(8,128)(2,1)}), bf16[8,64,2048]{2,1,0:T(8,128)(2,1)S(1)}, u32[]{:S(2)}, u32[]{:S(2)}) async-start(bf16[8,64,2048]{2,1,0:T(8,128)(2,1)} %dynamic-slice_dynamic-update-slice_fusion), calls=%async_computation | async-start | bytes 4194304 | tf_op jit(solution)/shard_map/all_to_all | solution.py:39
  (38 other events, 256.1 us)
Sparse Core Ops, SparseCore 0:
  108.3 131.4 reduce-scatter.1
where the time goes:
time: 250 us; the launch traced here: 249 us
  waiting for transfers between devices  70.9 us (28%)
  matrix products  39.6 us (16%)
  starting transfers between devices  36.7 us (15%)
  blocking collectives  28.4 us (11%)
  local copies, waits for them, and re-layouts  27.1 us (11%)
  Pallas kernels  24 us (10%)
  between operations  14.9 us (6%)
  other arithmetic  7.65 us (3%)
    all_gather x1, blocking collectives, step(): near = lax.all_gather(router_part, 'y', axis=0, tiled=False)  28.4 us
    ppermute x8, waiting for transfers between devices, shift(): return lax.ppermute(a, 'y', [(i, (i + step) % 4) for i in range(4)])  28.1 us
    unnamed x102, local copies, waits for them, and re-layouts  21.4 us
    pallas_call x1, Pallas kernels, weight_grads(): pl.pallas_call(functools.partial(grad_kernel, tiles), grid=(tiles + 4,),...  21.4 us
    reduce_scatter x1, waiting for transfers between devices, step(): lax.psum_scatter(parts.reshape(1, -1, parts.shape[2]), DP, scatter_dimens...  19.1 us
    ppermute x6, waiting for transfers between devices, ring_all(): lax.ppermute(a, axis, [(i, (i + k) % 4) for i in range(4)])  16.8 us
    dot_general x2, matrix products, dot_t(): lax.dot_general(a, b, (((1,), (1,)), ((), ())), preferred_element_type=F32)  12.5 us
    ppermute x6, starting transfers between devices, ring_all(): lax.ppermute(a, axis, [(i, (i + k) % 4) for i in range(4)])  12.2 us
  transfers between devices with their start and end apart: 27, of which 11 were waited for; matrix products, arithmetic and copies ran while one was open for 23% of the time, Pallas kernels for 0%

commit v1 on v0

--- a/solution.py
+++ b/solution.py
@@ -1,5 +1,3 @@
-import functools
-
 import jax
 import jax.numpy as jnp
 from jax import lax
@@ -24,7 +22,8 @@
 
 def spread(left, right):
     half = left.shape[0] // 2
-    return jnp.concatenate([shift(left[:half], 1), shift(right[half:], -1)], axis=0)
+    left, right = left[:half], right[half:]
+    return jnp.concatenate([shift(left, 1), shift(right, -1)], axis=0)
 
 
 def tdot(a, b):
@@ -47,34 +46,68 @@
 LANES = 128
 
 
-def grad_kernel(tiles, gate_a, gate_b, up_a, up_b, w_ref, xa_ref, xb_ref, dy_ref, prob_ref,
-                parts_ref, pre_ref, score_ref, hid, dyk, x):
+def in_hbm(a):
+    return pltpu.with_memory_space_constraint(a, pltpu.HBM)
+
+
+TILES = 6
+
+
+def gate_kernel(x_ref, gate_ref, up_ref, hid_ref, slope_ref, silu_ref):
+    x = x_ref[...]
+    gate = jnp.dot(x, gate_ref[...], preferred_element_type=F32)
+    up = jnp.dot(x, up_ref[...], preferred_element_type=F32)
+    sig = 1.0 / (1.0 + jnp.exp(-gate))
+    silu = gate * sig
+    hid_ref[...] = (silu * up).astype(BF)
+    slope_ref[...] = (up * sig * (1.0 + gate * (1.0 - sig))).astype(BF)
+    silu_ref[...] = silu.astype(BF)
+
+
+def gate_up(x, w):
+    rows, width = x.shape
+    ff = w.shape[1] // 2
+    tile = ff // TILES
+    w = in_hbm(w)
+    return pl.pallas_call(
+        gate_kernel,
+        grid=(TILES,),
+        in_specs=[
+            pl.BlockSpec((rows, width), lambda i: (0, 0)),
+            pl.BlockSpec((width, tile), lambda i: (0, i)),
+            pl.BlockSpec((width, tile), lambda i: (0, TILES + i)),
+        ],
+        out_specs=[pl.BlockSpec((rows, tile), lambda i: (0, i))] * 3,
+        out_shape=[pltpu.HBM((rows, ff), BF)] * 3,
+        compiler_params=pltpu.CompilerParams(vmem_limit_bytes=20 * 2**20),
+        cost_estimate=pl.CostEstimate(
+            flops=4 * rows * width * ff, bytes_accessed=2 * w.size, transcendentals=rows * ff
+        ),
+        name="gate_up",
+    )(x, w, w)
+
+
+def grad_kernel(hid_ref, slope_ref, silu_ref, w_ref, x, dy_ref, prob_ref,
+                parts_ref, pre_ref, score_ref, dyk, hid):
     i = pl.program_id(0)
     ff = hid.shape[1]
-    tile = gate_a.shape[1]
-    split = xa_ref.shape[0]
+    tile = ff // TILES
 
     @pl.when(i == 0)
     def _():
         score_ref[...] = jnp.zeros_like(score_ref)
         dyk[...] = (prob_ref[...] * dy_ref[...].astype(F32)).astype(BF)
-        x[:split, :] = xa_ref[...]
-        x[split:, :] = xb_ref[...]
-
-    @pl.when(i < tiles)
+
+    @pl.when(i < TILES)
     def _():
         at = pl.multiple_of(i * tile, tile)
         raw = lax.dot_general(dy_ref[...], w_ref[...], (((1,), (1,)), ((), ())), preferred_element_type=F32)
-        gate = jnp.concatenate([gate_a[...], gate_b[...]], axis=0)
-        up = jnp.concatenate([up_a[...], up_b[...]], axis=0)
-        sig = 1.0 / (1.0 + jnp.exp(-gate))
-        silu = gate * sig
-        hidden = (silu * up).astype(BF)
+        hidden = hid_ref[...]
         score_ref[...] += jnp.sum(hidden.astype(F32) * raw, axis=1, keepdims=True)
         grad = prob_ref[...] * raw
         hid[:, pl.ds(at, tile)] = hidden
-        pre_ref[:, pl.ds(at, tile)] = (grad * up * sig * (1.0 + gate * (1.0 - sig))).astype(BF)
-        pre_ref[:, pl.ds(pl.multiple_of(ff + at, tile), tile)] = (grad * silu).astype(BF)
+        pre_ref[:, pl.ds(at, tile)] = (grad * slope_ref[...].astype(F32)).astype(BF)
+        pre_ref[:, pl.ds(pl.multiple_of(ff + at, tile), tile)] = (grad * silu_ref[...].astype(F32)).astype(BF)
 
     def emit(left, right, base, r):
         cols = 512 if right.shape[1] % 512 == 0 else right.shape[1]
@@ -85,9 +118,9 @@
                 for d in range(4):
                     parts_ref[d, at : at + r, :] = g[d * r : (d + 1) * r, t * LANES : (t + 1) * LANES]
 
-    @pl.when(i >= tiles)
+    @pl.when(i >= TILES)
     def _():
-        k = i - tiles
+        k = i - TILES
         r = x.shape[1] // 16
         emit(x[:, pl.ds(pl.multiple_of(k * 4 * r, 4 * r), 4 * r)].T, pre_ref, 0, r)
         base = 2 * ff // LANES * r
@@ -95,33 +128,28 @@
         emit(hid[:, pl.ds(pl.multiple_of(k * 4 * r, 4 * r), 4 * r)].T, dyk, base, r)
 
 
-def weight_grads(act_a, act_b, w_dn, xa, xb, dy, row_prob):
+def weight_grads(acts, w_dn, x, dy, row_prob):
     rows, width = dy.shape
     ff = w_dn.shape[0]
-    tiles = 6
-    tile = ff // tiles
+    tile = ff // TILES
     depth = (2 * ff * (width // 16) + width * (ff // 16)) // LANES
-    na, nb = xa.shape[0], xb.shape[0]
-    last = tiles - 1
+    last = TILES - 1
     whole = lambda i: (0, 0)
-    low = lambda i: (0, jnp.minimum(i, last))
-    high = lambda i: (0, tiles + jnp.minimum(i, last))
+    across = pl.BlockSpec((rows, tile), lambda i: (0, jnp.minimum(i, last)))
     return pl.pallas_call(
-        functools.partial(grad_kernel, tiles),
-        grid=(tiles + 4,),
+        grad_kernel,
+        grid=(TILES + 4,),
         in_specs=[
-            pl.BlockSpec((na, tile), low),
-            pl.BlockSpec((nb, tile), low),
-            pl.BlockSpec((na, tile), high),
-            pl.BlockSpec((nb, tile), high),
+            across,
+            across,
+            across,
             pl.BlockSpec((tile, width), lambda i: (jnp.minimum(i, last), 0)),
-            pl.BlockSpec((na, width), whole),
-            pl.BlockSpec((nb, width), whole),
+            pl.BlockSpec((rows, width), whole),
             pl.BlockSpec((rows, width), whole),
             pl.BlockSpec((rows, 1), whole),
         ],
         out_specs=[
-            pl.BlockSpec((4, depth, LANES), lambda i: (jnp.maximum(i - tiles, 0), 0, 0)),
+            pl.BlockSpec((4, depth, LANES), lambda i: (jnp.maximum(i - TILES, 0), 0, 0)),
             pl.BlockSpec((rows, 2 * ff), whole),
             pl.BlockSpec((rows, 1), whole),
         ],
@@ -131,16 +159,15 @@
             jax.ShapeDtypeStruct((rows, 1), F32),
         ],
         scratch_shapes=[
+            pltpu.VMEM((rows, width), BF),
             pltpu.VMEM((rows, ff), BF),
-            pltpu.VMEM((rows, width), BF),
-            pltpu.VMEM((rows, width), BF),
         ],
         compiler_params=pltpu.CompilerParams(vmem_limit_bytes=36 * 2**20),
         cost_estimate=pl.CostEstimate(
-            flops=2 * rows * width * ff * 4, bytes_accessed=36 * 2**20, transcendentals=rows * ff
+            flops=2 * rows * width * ff * 4, bytes_accessed=36 * 2**20, transcendentals=0
         ),
         name="weight_grads",
-    )(act_a, act_b, act_a, act_b, w_dn, xa, xb, dy, row_prob)
+    )(*[in_hbm(v) for v in acts], in_hbm(w_dn), in_hbm(x), dy, row_prob)
 
 
 def unpack_kernel(in_ref, gu_ref, dn_ref):
@@ -159,6 +186,7 @@
             jax.ShapeDtypeStruct((width // 16, 2 * ff), BF),
             jax.ShapeDtypeStruct((ff // 16, width), BF),
         ],
+        compiler_params=pltpu.CompilerParams(vmem_limit_bytes=8 * 2**20),
         name="unpack",
     )(total)
 
@@ -223,17 +251,17 @@
 
     take_a = choose(x_parts[:6])
     xa = compact(take_a, x_parts[:6])
-    act_a = jnp.dot(xa, w_gu, preferred_element_type=F32)
     take_b = choose(x_parts[6:])
     xb = compact(take_b, x_parts[6:])
-    act_b = jnp.dot(xb, w_gu, preferred_element_type=F32)
+    x = jnp.concatenate([xa, xb], axis=0)
+    acts = gate_up(x, w_gu)
     take = jnp.concatenate([take_a, take_b], axis=0)
     pick = (jnp.arange(16, dtype=jnp.int32) % 8 == me)[None, :, None]
     pairs = jnp.stack([p[tok, : 16 * tok].reshape(16, tok) for p in g_parts]).astype(F32)
     prob_of = jnp.sum(jnp.where(pick, pairs, 0.0), axis=1)
     row_prob = jnp.sum(jnp.where(take, prob_of[:, None, :], 0.0), axis=2).reshape(8 * cap, 1)
     dy = compact(take, g_parts)
-    parts, pre, score = weight_grads(act_a, act_b, w_dn, xa, xb, dy, row_prob)
+    parts, pre, score = weight_grads(acts, w_dn, x, dy, row_prob)
     total = lax.psum_scatter(parts.reshape(1, -1, parts.shape[2]), DP, scatter_dimension=1, tiled=True)[0]
     gate_up_grad, down_grad = unpack(total, width, ff)
 

time: 250 us -> 244 us (0.976)
  matrix products: 39.6 us -> 24.7 us
  Pallas kernels: 24 us -> 37.8 us
  local copies, waits for them, and re-layouts: 27.1 us -> 21 us
    pallas_call x1 -> x2, Pallas kernels: 21.4 us -> 36.5 us  [the longest x1 23.6 us: weight_grads(): pl.pallas_call(grad_kernel, grid=(TILES + 4,), in_specs=[across, across,...]
    dot_general x2 -> x0, matrix products: 13.6 us -> none  [the longest x1 11.7 us: step(): act_a = jnp.dot(xa, w_gu, preferred_element_type=F32)]
    unnamed x102 -> x104, local copies, waits for them, and re-layouts: 21.4 us -> 15.4 us
  transfers between devices with their start and end apart: 27 -> 27, of which waited for: 11 -> 12; matrix products, arithmetic and copies ran while one was open for 23% -> 18% of each run, Pallas kernels for 0% -> 0%
where the time goes in v1:
time: 244 us; the launch traced here: 242 us
  waiting for transfers between devices  71.3 us (29%)
  Pallas kernels  37.8 us (15%)
  starting transfers between devices  36.4 us (15%)
  blocking collectives  28.5 us (12%)
  matrix products  24.7 us (10%)
  local copies, waits for them, and re-layouts  21 us (9%)
  between operations  15 us (6%)
  other arithmetic  7.7 us (3%)
    all_gather x1, blocking collectives, step(): near = lax.all_gather(router_part, 'y', axis=0, tiled=False)  28.5 us
    ppermute x8, waiting for transfers between devices, shift(): return lax.ppermute(a, 'y', [(i, (i + step) % 4) for i in range(4)])  28.1 us
    pallas_call x1, Pallas kernels, weight_grads(): pl.pallas_call(grad_kernel, grid=(TILES + 4,), in_specs=[across, across,...  23.6 us
    reduce_scatter x1, waiting for transfers between devices, step(): lax.psum_scatter(parts.reshape(1, -1, parts.shape[2]), DP, scatter_dimens...  19.5 us
    ppermute x6, waiting for transfers between devices, ring_all(): lax.ppermute(a, axis, [(i, (i + k) % 4) for i in range(4)])  16.7 us
    unnamed x104, local copies, waits for them, and re-layouts  15.4 us
    pallas_call x1, Pallas kernels, gate_up(): pl.pallas_call(gate_kernel, grid=(TILES,), in_specs=[pl.BlockSpec((rows,...  12.8 us
    dot_general x2, matrix products, dot_t(): lax.dot_general(a, b, (((1,), (1,)), ((), ())), preferred_element_type=F32)  12.7 us
  transfers between devices with their start and end apart: 27, of which 12 were waited for; matrix products, arithmetic and copies ran while one was open for 18% of the time, Pallas kernels for 0%

profile of v1, /device:TPU:0, one launch (start us, length us, event | category | flops | bytes accessed | tf_op | source)
XLA Modules:
  0.0 242.5 jit_solution(1476450402795654784)
XLA Ops:
  9.8 1.9 pad_maximum_fusion.3
  17.9 11.3 %collective-permute-done.11 = bf16[136,2048]{1,0:T(8,128)(2,1)} collective-permute-done((bf16[136,2048]{1,0:T(8,128)(2,1)}, bf16[136,2048]{1,0:T(8,128)(2,1)}, u32[]{:S(2)}, u32[]{:S(2)}) %collective-permute-start.11) | collective-permute-done | bytes 557088 | tf_op jit(solution)/shard_map/ppermute | solution.py:16
  30.3 2.8 %collective-permute-start.14 = (bf16[68,2048]{1,0:T(8,128)(2,1)S(1)}, bf16[68,2048]{1,0:T(8,128)(2,1)S(1)}, u32[]{:S(2)}, u32[]{:S(2)}) collective-permute-start(bf16[68,2048]{1,0:T(8,128)(2,1)S(1)} %slice.234), channel_id=1, source_target_pairs={{0,6},{2,0},{4,2},{6,4},{1,7},{3,1},{5,3},{7,5},{8,14},{10,8},{12,... | collective-permute-start | bytes 835592 | tf_op jit(solution)/shard_map/ppermute | solution.py:16
  33.2 7.9 %collective-permute-done.3 = bf16[136,2048]{1,0:T(8,128)(2,1)S(1)} collective-permute-done((bf16[136,2048]{1,0:T(8,128)(2,1)}, bf16[136,2048]{1,0:T(8,128)(2,1)S(1)}, u32[]{:S(2)}, u32[]{:S(2)}) %collective-permute-start.3) | collective-permute-done | bytes 557088 | tf_op jit(solution)/shard_map/ppermute | solution.py:16
  47.4 4.9 %collective-permute-done.5 = bf16[68,2048]{1,0:T(8,128)(2,1)S(1)} collective-permute-done((bf16[68,2048]{1,0:T(8,128)(2,1)S(1)}, bf16[68,2048]{1,0:T(8,128)(2,1)S(1)}, u32[]{:S(2)}, u32[]{:S(2)}) %collective-permute-start.5) | collective-permute-done | bytes 278560 | tf_op jit(solution)/shard_map/ppermute | solution.py:16
  52.3 2.6 %collective-permute-done.6 = bf16[68,2048]{1,0:T(8,128)(2,1)S(1)} collective-permute-done((bf16[68,2048]{1,0:T(8,128)(2,1)S(1)}, bf16[68,2048]{1,0:T(8,128)(2,1)S(1)}, u32[]{:S(2)}, u32[]{:S(2)}) %collective-permute-start.6) | collective-permute-done | bytes 278560 | tf_op jit(solution)/shard_map/ppermute | solution.py:16
  64.7 12.8 %gate_up.1 = (bf16[512,1536]{1,0:T(8,128)(2,1)}, bf16[512,1536]{1,0:T(8,128)(2,1)}, bf16[512,1536]{1,0:T(8,128)(2,1)}) custom-call(bf16[512,2048]{1,0:T(8,128)(2,1)S(1)} %fusion.9.x_ref.x, bf16[2048,3072]{1,0:T(8,128)(2,1)} %bitcast.178, bf16[2048,3072]{1,0:T(8,128)(2,1)} %bitcast.179), custom_call_target="tpu_custom_call" | custom-call | flops 6442450944 | bytes 12582912 | tf_op jit(solution)/shard_map/gate_up/pallas_call | solution.py:72
  78.1 23.6 %weight_grads.1 = (bf16[16,4608,128]{2,1,0:T(8,128)(2,1)}, bf16[512,3072]{1,0:T(8,128)(2,1)}, f32[512,1]{1,0:T(8,128)S(1)}) custom-call(bf16[512,1536]{1,0:T(8,128)(2,1)} %get-tuple-element.12.hid_ref, bf16[512,1536]{1,0:T(8,128)(2,1)} %get-tuple-element.13.slope_ref, bf16[512,1536]{1,0:T(8,128)(2,1)} %get-tuple-element.14.silu_ref, ...), custom_call_target="tpu_custom_call" | custom-call | flops 12884901888 | bytes 37748736 | tf_op jit(solution)/shard_map/weight_grads/pallas_call | solution.py:139
  108.9 3.3 %all-to-all-start.1 = ((f32[8,1,64]{2,1,0:T(1,128)}), f32[8,1,64]{2,1,0:T(1,128)S(1)}, u32[]{:S(2)}, u32[]{:S(2)}) async-start(f32[8,1,64]{2,1,0:T(1,128)} %bitcast.22), calls=%async_computation.1 | async-start | bytes 8192 | tf_op jit(solution)/shard_map/all_to_all | solution.py:38
  112.2 10.8 %convolution_convert_fusion = bf16[512,2048]{1,0:T(8,128)(2,1)S(1)} fusion(bf16[512,3072]{1,0:T(8,128)(2,1)} %get-tuple-element.15, bf16[1,2048,3072]{2,1,0:T(8,128)(2,1)} %param.12), kind=kOutput, calls=%fused_computation | convolution fusion | flops 6443499520 | bytes 17825792 | tf_op jit(solution)/shard_map/dot_general | solution.py:34
  128.4 4.6 %all-to-all-start.2 = ((bf16[8,16,128]{2,1,0:T(8,128)(2,1)}), bf16[8,16,128]{2,1,0:T(8,128)(2,1)S(1)}, u32[]{:S(2)}, u32[]{:S(2)}) async-start(bf16[8,16,128]{2,1,0:T(8,128)(2,1)} %bitcast.26), calls=%async_computation.2 | async-start | bytes 65536 | tf_op jit(solution)/shard_map/all_to_all | solution.py:38
  133.8 4.7 %all-to-all-done.2 = bf16[8,16,128]{2,1,0:T(8,128)(2,1)S(1)} async-done(((bf16[8,16,128]{2,1,0:T(8,128)(2,1)}), bf16[8,16,128]{2,1,0:T(8,128)(2,1)S(1)}, u32[]{:S(2)}, u32[]{:S(2)}) %all-to-all-start.2) | async-done | bytes 32800 | tf_op jit(solution)/shard_map/all_to_all | solution.py:38
  138.6 3.0 %fusion.78 = f32[16,2048]{1,0:T(8,128)S(1)} fusion(bf16[16,1024]{1,0:T(8,128)(2,1)S(1)} %constant_dynamic-update-slice_fusion.14, bf16[1024,2048]{1,0:T(8,128)(2,1)} %slice_dynamic-update-slice_fusion), kind=kOutput, calls=%fused_computation.218 | convolution fusion | flops 67108864 | bytes 4358144 | tf_op jit(solution)/shard_map/dot_general | solution.py:286
  142.9 2.7 %collective-permute-start.17 = (f32[16,2048]{1,0:T(8,128)S(1)}, f32[16,2048]{1,0:T(8,128)S(1)}, u32[]{:S(2)}, u32[]{:S(2)}) collective-permute-start(f32[16,2048]{1,0:T(8,128)S(1)} %fusion.78), channel_id=1, source_target_pairs={{0,64},{32,96},{64,0},{96,32},{1,65},{33,97},{65,1},{97,33},{2,66}... | collective-permute-start | bytes 393224 | tf_op jit(solution)/shard_map/ppermute | solution.py:42
  147.8 3.7 %collective-permute-done.16 = f32[16,2048]{1,0:T(8,128)S(1)} collective-permute-done((f32[16,2048]{1,0:T(8,128)S(1)}, f32[16,2048]{1,0:T(8,128)S(1)}, u32[]{:S(2)}, u32[]{:S(2)}) %collective-permute-start.16) | collective-permute-done | bytes 131104 | tf_op jit(solution)/shard_map/ppermute | solution.py:42
  151.6 6.5 %collective-permute-done.17 = f32[16,2048]{1,0:T(8,128)S(1)} collective-permute-done((f32[16,2048]{1,0:T(8,128)S(1)}, f32[16,2048]{1,0:T(8,128)S(1)}, u32[]{:S(2)}, u32[]{:S(2)}) %collective-permute-start.17) | collective-permute-done | bytes 131104 | tf_op jit(solution)/shard_map/ppermute | solution.py:42
  158.1 2.0 collective-permute-start.19
  160.1 3.6 %collective-permute-start.20 = (f32[16,2048]{1,0:T(8,128)S(1)}, f32[16,2048]{1,0:T(8,128)S(1)}, u32[]{:S(2)}, u32[]{:S(2)}) collective-permute-start(f32[16,2048]{1,0:T(8,128)S(1)} %add_add_fusion.1), channel_id=1, source_target_pairs={{0,16},{8,24},{16,0},{24,8},{1,17},{9,25},{17,1},{25,9},{2,18},{10... | collective-permute-start | bytes 393224 | tf_op jit(solution)/shard_map/ppermute | solution.py:42
  165.4 3.6 %all-to-all-start = ((bf16[8,64,2048]{2,1,0:T(8,128)(2,1)}), bf16[8,64,2048]{2,1,0:T(8,128)(2,1)S(1)}, u32[]{:S(2)}, u32[]{:S(2)}) async-start(bf16[8,64,2048]{2,1,0:T(8,128)(2,1)} %dynamic-slice_dynamic-update-slice_fusion), calls=%async_computation | async-start | bytes 4194304 | tf_op jit(solution)/shard_map/all_to_all | solution.py:38
  169.0 6.4 %collective-permute-done.20 = f32[16,2048]{1,0:T(8,128)S(1)} collective-permute-done((f32[16,2048]{1,0:T(8,128)S(1)}, f32[16,2048]{1,0:T(8,128)S(1)}, u32[]{:S(2)}, u32[]{:S(2)}) %collective-permute-start.20) | collective-permute-done | bytes 131104 | tf_op jit(solution)/shard_map/ppermute | solution.py:42
  175.5 28.5 %all-gather = f32[64,2048]{1,0:T(8,128)S(1)} all-gather(f32[16,2048]{1,0:T(8,128)S(1)} %add_add_fusion), channel_id=2, replica_groups=mesh['x'=4,'z'=4,'y'=4,'c'=2] {'y'}, dimensions={0}, use_global_device_ids=true | all-gather | bytes 655360 | tf_op jit(solution)/shard_map/all_gather | solution.py:288
  204.0 2.0 collective-permute-done.22
  208.4 2.8 %copy.18 = f32[2048,128]{1,0:T(8,128)} copy(f32[2048,128]{0,1:T(8,128)} %bitcast.181) | data formatting | bytes 2097152
  213.5 19.5 %reduce-scatter.2.cloned.1.call-done = bf16[1,4608,128]{2,1,0:T(8,128)(2,1)} async-done(((bf16[1,73728,128]{2,1,0:T(8,128)(2,1)}), bf16[1,4608,128]{2,1,0:T(8,128)(2,1)}) %reduce-scatter.2.cloned.1.call-update) | async-done | bytes 1179664 | tf_op jit(solution)/shard_map/reduce_scatter | solution.py:265
  (224 shorter events, 51.6 us)
Async XLA Ops:
  7.2 225.9 %reduce-scatter.2.cloned.1.call-start = ((), (), s32[]{:S(2)}) async-start(), calls=%async_computation.4 | async-start | bytes 20054016 | tf_op jit(solution)/shard_map/reduce_scatter | solution.py:265
  11.7 18.6 %collective-permute-start.9 = (bf16[136,2048]{1,0:T(8,128)(2,1)}, bf16[136,2048]{1,0:T(8,128)(2,1)S(1)}, u32[]{:S(2)}, u32[]{:S(2)}) collective-permute-start(bf16[136,2048]{1,0:T(8,128)(2,1)} %pad_maximum_fusion.3), channel_id=1, source_target_pairs={{0,2},{2,4},{4,6},{6,0},{1,3},{3,5},{5,7},{7,1},{8,10},{10,12},{12... | collective-permute-start | bytes 1671176 | tf_op jit(solution)/shard_map/ppermute | solution.py:16
  13.4 15.8 %collective-permute-start.11 = (bf16[136,2048]{1,0:T(8,128)(2,1)}, bf16[136,2048]{1,0:T(8,128)(2,1)}, u32[]{:S(2)}, u32[]{:S(2)}) collective-permute-start(bf16[136,2048]{1,0:T(8,128)(2,1)} %pad_maximum_fusion.3), channel_id=1, source_target_pairs={{0,6},{2,0},{4,2},{6,4},{1,7},{3,1},{5,3},{7,5},{8,14},{10,8},{12,... | collective-permute-start | bytes 1671176 | tf_op jit(solution)/shard_map/ppermute | solution.py:16
  15.8 25.2 %collective-permute-start.3 = (bf16[136,2048]{1,0:T(8,128)(2,1)}, bf16[136,2048]{1,0:T(8,128)(2,1)S(1)}, u32[]{:S(2)}, u32[]{:S(2)}) collective-permute-start(bf16[136,2048]{1,0:T(8,128)(2,1)} %fusion.18), channel_id=1, source_target_pairs={{0,6},{2,0},{4,2},{6,4},{1,7},{3,1},{5,3},{7,5},{8,14},{10,8},{12,... | collective-permute-start | bytes 1671176 | tf_op jit(solution)/shard_map/ppermute | solution.py:16
  17.8 25.0 %collective-permute-start.1 = (bf16[136,2048]{1,0:T(8,128)(2,1)}, bf16[136,2048]{1,0:T(8,128)(2,1)S(1)}, u32[]{:S(2)}, u32[]{:S(2)}) collective-permute-start(bf16[136,2048]{1,0:T(8,128)(2,1)} %fusion.18), channel_id=1, source_target_pairs={{0,2},{2,4},{4,6},{6,0},{1,3},{3,5},{5,7},{7,1},{8,10},{10,12},{12... | collective-permute-start | bytes 1671176 | tf_op jit(solution)/shard_map/ppermute | solution.py:16
  17.9 26.6 %collective-permute-start = (bf16[136,2048]{1,0:T(8,128)(2,1)}, bf16[136,2048]{1,0:T(8,128)(2,1)S(1)}, u32[]{:S(2)}, u32[]{:S(2)}) collective-permute-start(bf16[136,2048]{1,0:T(8,128)(2,1)} %fusion.18), channel_id=1, source_target_pairs={{0,1},{1,0},{2,3},{3,2},{4,5},{5,4},{6,7},{7,6},{8,9},{9,8},{10,11... | collective-permute-start | bytes 1671176 | tf_op jit(solution)/shard_map/ppermute | solution.py:20
  29.2 15.8 %collective-permute-start.8 = (bf16[136,2048]{1,0:T(8,128)(2,1)}, bf16[136,2048]{1,0:T(8,128)(2,1)S(1)}, u32[]{:S(2)}, u32[]{:S(2)}) collective-permute-start(bf16[136,2048]{1,0:T(8,128)(2,1)} %pad_maximum_fusion.3), channel_id=1, source_target_pairs={{0,1},{1,0},{2,3},{3,2},{4,5},{5,4},{6,7},{7,6},{8,9},{9,8},{10,11... | collective-permute-start | bytes 1671176 | tf_op jit(solution)/shard_map/ppermute | solution.py:20
  30.3 17.1 %collective-permute-start.14 = (bf16[68,2048]{1,0:T(8,128)(2,1)S(1)}, bf16[68,2048]{1,0:T(8,128)(2,1)S(1)}, u32[]{:S(2)}, u32[]{:S(2)}) collective-permute-start(bf16[68,2048]{1,0:T(8,128)(2,1)S(1)} %slice.234), channel_id=1, source_target_pairs={{0,6},{2,0},{4,2},{6,4},{1,7},{3,1},{5,3},{7,5},{8,14},{10,8},{12,... | collective-permute-start | bytes 835592 | tf_op jit(solution)/shard_map/ppermute | solution.py:16
  41.1 14.0 %collective-permute-start.13 = (bf16[68,2048]{1,0:T(8,128)(2,1)S(1)}, bf16[68,2048]{1,0:T(8,128)(2,1)S(1)}, u32[]{:S(2)}, u32[]{:S(2)}) collective-permute-start(bf16[68,2048]{1,0:T(8,128)(2,1)S(1)} %slice.233), channel_id=1, source_target_pairs={{0,2},{2,4},{4,6},{6,0},{1,3},{3,5},{5,7},{7,1},{8,10},{10,12},{12... | collective-permute-start | bytes 835592 | tf_op jit(solution)/shard_map/ppermute | solution.py:16
  42.7 9.5 %collective-permute-start.5 = (bf16[68,2048]{1,0:T(8,128)(2,1)S(1)}, bf16[68,2048]{1,0:T(8,128)(2,1)S(1)}, u32[]{:S(2)}, u32[]{:S(2)}) collective-permute-start(bf16[68,2048]{1,0:T(8,128)(2,1)S(1)} %slice.218), channel_id=1, source_target_pairs={{0,6},{2,0},{4,2},{6,4},{1,7},{3,1},{5,3},{7,5},{8,14},{10,8},{12,... | collective-permute-start | bytes 835592 | tf_op jit(solution)/shard_map/ppermute | solution.py:16
  44.5 10.4 %collective-permute-start.6 = (bf16[68,2048]{1,0:T(8,128)(2,1)S(1)}, bf16[68,2048]{1,0:T(8,128)(2,1)S(1)}, u32[]{:S(2)}, u32[]{:S(2)}) collective-permute-start(bf16[68,2048]{1,0:T(8,128)(2,1)S(1)} %slice.220), channel_id=1, source_target_pairs={{0,2},{2,4},{4,6},{6,0},{1,3},{3,5},{5,7},{7,1},{8,10},{10,12},{12... | collective-permute-start | bytes 835592 | tf_op jit(solution)/shard_map/ppermute | solution.py:16
  45.1 10.6 %collective-permute-start.2 = (bf16[136,2048]{1,0:T(8,128)(2,1)S(1)}, bf16[136,2048]{1,0:T(8,128)(2,1)S(1)}, u32[]{:S(2)}, u32[]{:S(2)}) collective-permute-start(bf16[136,2048]{1,0:T(8,128)(2,1)S(1)} %collective-permute-done.1), channel_id=1, source_target_pairs={{0,1},{1,0},{2,3},{3,2},{4,5},{5,4},{6,7},{7,6},{8,9},{9,8},{10,11... | collective-permute-start | bytes 1671176 | tf_op jit(solution)/shard_map/ppermute | solution.py:20
  47.4 8.7 %collective-permute-start.4 = (bf16[136,2048]{1,0:T(8,128)(2,1)S(1)}, bf16[136,2048]{1,0:T(8,128)(2,1)S(1)}, u32[]{:S(2)}, u32[]{:S(2)}) collective-permute-start(bf16[136,2048]{1,0:T(8,128)(2,1)S(1)} %collective-permute-done.3), channel_id=1, source_target_pairs={{0,1},{1,0},{2,3},{3,2},{4,5},{5,4},{6,7},{7,6},{8,9},{9,8},{10,11... | collective-permute-start | bytes 1671176 | tf_op jit(solution)/shard_map/ppermute | solution.py:20
  55.1 5.6 %collective-permute-start.7 = (bf16[136,2048]{1,0:T(8,128)(2,1)S(1)}, bf16[136,2048]{1,0:T(8,128)(2,1)S(1)}, u32[]{:S(2)}, u32[]{:S(2)}) collective-permute-start(bf16[136,2048]{1,0:T(8,128)(2,1)S(1)} %pad_maximum_fusion.1), channel_id=1, source_target_pairs={{0,1},{1,0},{2,3},{3,2},{4,5},{5,4},{6,7},{7,6},{8,9},{9,8},{10,11... | collective-permute-start | bytes 1671176 | tf_op jit(solution)/shard_map/ppermute | solution.py:20
  55.8 5.2 %collective-permute-start.15 = (bf16[136,2048]{1,0:T(8,128)(2,1)S(1)}, bf16[136,2048]{1,0:T(8,128)(2,1)S(1)}, u32[]{:S(2)}, u32[]{:S(2)}) collective-permute-start(bf16[136,2048]{1,0:T(8,128)(2,1)S(1)} %pad_maximum_fusion.2), channel_id=1, source_target_pairs={{0,1},{1,0},{2,3},{3,2},{4,5},{5,4},{6,7},{7,6},{8,9},{9,8},{10,11... | collective-permute-start | bytes 1671176 | tf_op jit(solution)/shard_map/ppermute | solution.py:20
  108.9 18.6 %all-to-all-start.1 = ((f32[8,1,64]{2,1,0:T(1,128)}), f32[8,1,64]{2,1,0:T(1,128)S(1)}, u32[]{:S(2)}, u32[]{:S(2)}) async-start(f32[8,1,64]{2,1,0:T(1,128)} %bitcast.22), calls=%async_computation.1 | async-start | bytes 8192 | tf_op jit(solution)/shard_map/all_to_all | solution.py:38
  128.4 10.1 %all-to-all-start.2 = ((bf16[8,16,128]{2,1,0:T(8,128)(2,1)}), bf16[8,16,128]{2,1,0:T(8,128)(2,1)S(1)}, u32[]{:S(2)}, u32[]{:S(2)}) async-start(bf16[8,16,128]{2,1,0:T(8,128)(2,1)} %bitcast.26), calls=%async_computation.2 | async-start | bytes 65536 | tf_op jit(solution)/shard_map/all_to_all | solution.py:38
  141.6 10.0 %collective-permute-start.16 = (f32[16,2048]{1,0:T(8,128)S(1)}, f32[16,2048]{1,0:T(8,128)S(1)}, u32[]{:S(2)}, u32[]{:S(2)}) collective-permute-start(f32[16,2048]{1,0:T(8,128)S(1)} %fusion.78), channel_id=1, source_target_pairs={{0,32},{32,64},{64,96},{96,0},{1,33},{33,65},{65,97},{97,1},{2,34}... | collective-permute-start | bytes 393224 | tf_op jit(solution)/shard_map/ppermute | solution.py:42
  142.9 15.1 %collective-permute-start.17 = (f32[16,2048]{1,0:T(8,128)S(1)}, f32[16,2048]{1,0:T(8,128)S(1)}, u32[]{:S(2)}, u32[]{:S(2)}) collective-permute-start(f32[16,2048]{1,0:T(8,128)S(1)} %fusion.78), channel_id=1, source_target_pairs={{0,64},{32,96},{64,0},{96,32},{1,65},{33,97},{65,1},{97,33},{2,66}... | collective-permute-start | bytes 393224 | tf_op jit(solution)/shard_map/ppermute | solution.py:42
  145.7 12.4 %collective-permute-start.18 = (f32[16,2048]{1,0:T(8,128)S(1)}, f32[16,2048]{1,0:T(8,128)S(1)}, u32[]{:S(2)}, u32[]{:S(2)}) collective-permute-start(f32[16,2048]{1,0:T(8,128)S(1)} %fusion.78), channel_id=1, source_target_pairs={{0,96},{32,0},{64,32},{96,64},{1,97},{33,1},{65,33},{97,65},{2,98}... | collective-permute-start | bytes 393224 | tf_op jit(solution)/shard_map/ppermute | solution.py:42
  158.1 10.9 %collective-permute-start.19 = (f32[16,2048]{1,0:T(8,128)S(1)}, f32[16,2048]{1,0:T(8,128)S(1)}, u32[]{:S(2)}, u32[]{:S(2)}) collective-permute-start(f32[16,2048]{1,0:T(8,128)S(1)} %add_add_fusion.1), channel_id=1, source_target_pairs={{0,8},{8,16},{16,24},{24,0},{1,9},{9,17},{17,25},{25,1},{2,10},{10... | collective-permute-start | bytes 393224 | tf_op jit(solution)/shard_map/ppermute | solution.py:42
  160.1 15.4 %collective-permute-start.20 = (f32[16,2048]{1,0:T(8,128)S(1)}, f32[16,2048]{1,0:T(8,128)S(1)}, u32[]{:S(2)}, u32[]{:S(2)}) collective-permute-start(f32[16,2048]{1,0:T(8,128)S(1)} %add_add_fusion.1), channel_id=1, source_target_pairs={{0,16},{8,24},{16,0},{24,8},{1,17},{9,25},{17,1},{25,9},{2,18},{10... | collective-permute-start | bytes 393224 | tf_op jit(solution)/shard_map/ppermute | solution.py:42
  163.7 11.8 %collective-permute-start.21 = (f32[16,2048]{1,0:T(8,128)S(1)}, f32[16,2048]{1,0:T(8,128)S(1)}, u32[]{:S(2)}, u32[]{:S(2)}) collective-permute-start(f32[16,2048]{1,0:T(8,128)S(1)} %add_add_fusion.1), channel_id=1, source_target_pairs={{0,24},{8,0},{16,8},{24,16},{1,25},{9,1},{17,9},{25,17},{2,26},{10... | collective-permute-start | bytes 393224 | tf_op jit(solution)/shard_map/ppermute | solution.py:42
  165.4 45.7 %all-to-all-start = ((bf16[8,64,2048]{2,1,0:T(8,128)(2,1)}), bf16[8,64,2048]{2,1,0:T(8,128)(2,1)S(1)}, u32[]{:S(2)}, u32[]{:S(2)}) async-start(bf16[8,64,2048]{2,1,0:T(8,128)(2,1)} %dynamic-slice_dynamic-update-slice_fusion), calls=%async_computation | async-start | bytes 4194304 | tf_op jit(solution)/shard_map/all_to_all | solution.py:38
  (39 other events, 245.7 us)
Sparse Core Ops, SparseCore 0:
  101.8 131.1 reduce-scatter.1

commit v2 on v1

--- a/solution.py
+++ b/solution.py
@@ -21,7 +21,7 @@
 
 
 def spread(left, right):
-    half = left.shape[0] // 2
+    half = left.shape[0] // 16 * 8
     left, right = left[:half], right[half:]
     return jnp.concatenate([shift(left, 1), shift(right, -1)], axis=0)
 
@@ -53,61 +53,33 @@
 TILES = 6
 
 
-def gate_kernel(x_ref, gate_ref, up_ref, hid_ref, slope_ref, silu_ref):
-    x = x_ref[...]
-    gate = jnp.dot(x, gate_ref[...], preferred_element_type=F32)
-    up = jnp.dot(x, up_ref[...], preferred_element_type=F32)
-    sig = 1.0 / (1.0 + jnp.exp(-gate))
-    silu = gate * sig
-    hid_ref[...] = (silu * up).astype(BF)
-    slope_ref[...] = (up * sig * (1.0 + gate * (1.0 - sig))).astype(BF)
-    silu_ref[...] = silu.astype(BF)
-
-
-def gate_up(x, w):
-    rows, width = x.shape
-    ff = w.shape[1] // 2
-    tile = ff // TILES
-    w = in_hbm(w)
-    return pl.pallas_call(
-        gate_kernel,
-        grid=(TILES,),
-        in_specs=[
-            pl.BlockSpec((rows, width), lambda i: (0, 0)),
-            pl.BlockSpec((width, tile), lambda i: (0, i)),
-            pl.BlockSpec((width, tile), lambda i: (0, TILES + i)),
-        ],
-        out_specs=[pl.BlockSpec((rows, tile), lambda i: (0, i))] * 3,
-        out_shape=[pltpu.HBM((rows, ff), BF)] * 3,
-        compiler_params=pltpu.CompilerParams(vmem_limit_bytes=20 * 2**20),
-        cost_estimate=pl.CostEstimate(
-            flops=4 * rows * width * ff, bytes_accessed=2 * w.size, transcendentals=rows * ff
-        ),
-        name="gate_up",
-    )(x, w, w)
-
-
-def grad_kernel(hid_ref, slope_ref, silu_ref, w_ref, x, dy_ref, prob_ref,
-                parts_ref, pre_ref, score_ref, dyk, hid):
+def expert_kernel(w_gate, w_up, w_dn, x, dy, prob_ref, parts_ref, pre_hbm, score_ref, dyk, hid, pre, sem):
     i = pl.program_id(0)
     ff = hid.shape[1]
     tile = ff // TILES
+    store = pltpu.make_async_copy(pre, pre_hbm, sem)
 
     @pl.when(i == 0)
     def _():
         score_ref[...] = jnp.zeros_like(score_ref)
-        dyk[...] = (prob_ref[...] * dy_ref[...].astype(F32)).astype(BF)
+        dyk[...] = (prob_ref[...] * dy[...].astype(F32)).astype(BF)
 
     @pl.when(i < TILES)
     def _():
-        at = pl.multiple_of(i * tile, tile)
-        raw = lax.dot_general(dy_ref[...], w_ref[...], (((1,), (1,)), ((), ())), preferred_element_type=F32)
-        hidden = hid_ref[...]
+        here = pl.ds(pl.multiple_of(i * tile, tile), tile)
+        there = pl.ds(pl.multiple_of(ff + i * tile, tile), tile)
+        rows = x[...]
+        gate = jnp.dot(rows, w_gate[...], preferred_element_type=F32)
+        up = jnp.dot(rows, w_up[...], preferred_element_type=F32)
+        raw = lax.dot_general(dy[...], w_dn[...], (((1,), (1,)), ((), ())), preferred_element_type=F32)
+        sig = 1.0 / (1.0 + jnp.exp(-gate))
+        silu = gate * sig
+        hidden = (silu * up).astype(BF)
         score_ref[...] += jnp.sum(hidden.astype(F32) * raw, axis=1, keepdims=True)
         grad = prob_ref[...] * raw
-        hid[:, pl.ds(at, tile)] = hidden
-        pre_ref[:, pl.ds(at, tile)] = (grad * slope_ref[...].astype(F32)).astype(BF)
-        pre_ref[:, pl.ds(pl.multiple_of(ff + at, tile), tile)] = (grad * silu_ref[...].astype(F32)).astype(BF)
+        hid[:, here] = hidden
+        pre[:, here] = (grad * up * sig * (1.0 + gate * (1.0 - sig))).astype(BF)
+        pre[:, there] = (grad * silu).astype(BF)
 
     def emit(left, right, base, r):
         cols = 512 if right.shape[1] % 512 == 0 else right.shape[1]
@@ -118,39 +90,44 @@
                 for d in range(4):
                     parts_ref[d, at : at + r, :] = g[d * r : (d + 1) * r, t * LANES : (t + 1) * LANES]
 
+    @pl.when(i == TILES)
+    def _():
+        store.start()
+
     @pl.when(i >= TILES)
     def _():
         k = i - TILES
         r = x.shape[1] // 16
-        emit(x[:, pl.ds(pl.multiple_of(k * 4 * r, 4 * r), 4 * r)].T, pre_ref, 0, r)
+        emit(x[:, pl.ds(pl.multiple_of(k * 4 * r, 4 * r), 4 * r)].T, pre, 0, r)
         base = 2 * ff // LANES * r
         r = ff // 16
         emit(hid[:, pl.ds(pl.multiple_of(k * 4 * r, 4 * r), 4 * r)].T, dyk, base, r)
 
-
-def weight_grads(acts, w_dn, x, dy, row_prob):
+    @pl.when(i == TILES + 3)
+    def _():
+        store.wait()
+
+
+def expert_grads(w_gu, w_dn, x, dy, row_prob):
     rows, width = dy.shape
     ff = w_dn.shape[0]
-    tile = ff // TILES
     depth = (2 * ff * (width // 16) + width * (ff // 16)) // LANES
-    last = TILES - 1
+    tile, last = ff // TILES, TILES - 1
     whole = lambda i: (0, 0)
-    across = pl.BlockSpec((rows, tile), lambda i: (0, jnp.minimum(i, last)))
+    w_gu = in_hbm(w_gu)
     return pl.pallas_call(
-        grad_kernel,
+        expert_kernel,
         grid=(TILES + 4,),
         in_specs=[
-            across,
-            across,
-            across,
+            pl.BlockSpec((width, tile), lambda i: (0, jnp.minimum(i, last))),
+            pl.BlockSpec((width, tile), lambda i: (0, TILES + jnp.minimum(i, last))),
             pl.BlockSpec((tile, width), lambda i: (jnp.minimum(i, last), 0)),
-            pl.BlockSpec((rows, width), whole),
-            pl.BlockSpec((rows, width), whole),
-            pl.BlockSpec((rows, 1), whole),
-        ],
+        ]
+        + [pl.BlockSpec((rows, width), whole, pipeline_mode=pl.Buffered(1))] * 2
+        + [pl.BlockSpec((rows, 1), whole)],
         out_specs=[
             pl.BlockSpec((4, depth, LANES), lambda i: (jnp.maximum(i - TILES, 0), 0, 0)),
-            pl.BlockSpec((rows, 2 * ff), whole),
+            pl.BlockSpec(memory_space=pltpu.HBM),
             pl.BlockSpec((rows, 1), whole),
         ],
         out_shape=[
@@ -161,13 +138,15 @@
         scratch_shapes=[
             pltpu.VMEM((rows, width), BF),
             pltpu.VMEM((rows, ff), BF),
+            pltpu.VMEM((rows, 2 * ff), BF),
+            pltpu.SemaphoreType.DMA,
         ],
         compiler_params=pltpu.CompilerParams(vmem_limit_bytes=36 * 2**20),
         cost_estimate=pl.CostEstimate(
-            flops=2 * rows * width * ff * 4, bytes_accessed=36 * 2**20, transcendentals=0
+            flops=16 * rows * width * ff, bytes_accessed=40 * 2**20, transcendentals=rows * ff
         ),
-        name="weight_grads",
-    )(*[in_hbm(v) for v in acts], in_hbm(w_dn), in_hbm(x), dy, row_prob)
+        name="expert_grads",
+    )(w_gu, w_gu, in_hbm(w_dn), in_hbm(x), in_hbm(dy), row_prob)
 
 
 def unpack_kernel(in_ref, gu_ref, dn_ref):
@@ -254,14 +233,13 @@
     take_b = choose(x_parts[6:])
     xb = compact(take_b, x_parts[6:])
     x = jnp.concatenate([xa, xb], axis=0)
-    acts = gate_up(x, w_gu)
     take = jnp.concatenate([take_a, take_b], axis=0)
     pick = (jnp.arange(16, dtype=jnp.int32) % 8 == me)[None, :, None]
     pairs = jnp.stack([p[tok, : 16 * tok].reshape(16, tok) for p in g_parts]).astype(F32)
     prob_of = jnp.sum(jnp.where(pick, pairs, 0.0), axis=1)
     row_prob = jnp.sum(jnp.where(take, prob_of[:, None, :], 0.0), axis=2).reshape(8 * cap, 1)
     dy = compact(take, g_parts)
-    parts, pre, score = weight_grads(acts, w_dn, x, dy, row_prob)
+    parts, pre, score = expert_grads(w_gu, w_dn, x, dy, row_prob)
     total = lax.psum_scatter(parts.reshape(1, -1, parts.shape[2]), DP, scatter_dimension=1, tiled=True)[0]
     gate_up_grad, down_grad = unpack(total, width, ff)
 

time: 244 us -> 239 us (0.980)
  Pallas kernels: 37.8 us -> 30.7 us
  matrix products: 24.7 us -> 29 us
  starting transfers between devices: 36.4 us -> 33.3 us
  local copies, waits for them, and re-layouts: 21 us -> 23.7 us
    pallas_call x2 -> x1, Pallas kernels: 36.5 us -> 29.4 us  [expert_grads(): pl.pallas_call(expert_kernel, grid=(TILES + 4,), in_specs=[pl.BlockSpec((...]
    dot_general x16, matrix products: 6.81 us -> 10.7 us  [compact(): jnp.dot(take[j].astype(BF), p[:tok], preferred_element_type=F32).astype(BF)]
    ppermute x8, waiting for transfers between devices: 28.1 us -> 24.8 us  [shift(): return lax.ppermute(a, 'y', [(i, (i + step) % 4) for i in range(4)])]
    unnamed x104 -> x87, local copies, waits for them, and re-layouts: 15.4 us -> 16.4 us
  transfers between devices with their start and end apart: 27 -> 27, of which waited for: 12 -> 16; matrix products, arithmetic and copies ran while one was open for 18% -> 21% of each run, Pallas kernels for 0% -> 0%
where the time goes in v2:
time: 239 us; the launch traced here: 238 us
  waiting for transfers between devices  70.2 us (29%)
  starting transfers between devices  33.3 us (14%)
  Pallas kernels  30.7 us (13%)
  matrix products  29 us (12%)
  blocking collectives  28.4 us (12%)
  local copies, waits for them, and re-layouts  23.7 us (10%)
  between operations  14.9 us (6%)
  other arithmetic  7.93 us (3%)
    pallas_call x1, Pallas kernels, expert_grads(): pl.pallas_call(expert_kernel, grid=(TILES + 4,), in_specs=[pl.BlockSpec((...  29.4 us
    all_gather x1, blocking collectives, step(): near = lax.all_gather(router_part, 'y', axis=0, tiled=False)  28.4 us
    ppermute x8, waiting for transfers between devices, shift(): return lax.ppermute(a, 'y', [(i, (i + step) % 4) for i in range(4)])  24.8 us
    reduce_scatter x1, waiting for transfers between devices, step(): lax.psum_scatter(parts.reshape(1, -1, parts.shape[2]), DP, scatter_dimens...  20.4 us
    ppermute x6, waiting for transfers between devices, ring_all(): lax.ppermute(a, axis, [(i, (i + k) % 4) for i in range(4)])  17.1 us
    unnamed x87, local copies, waits for them, and re-layouts  16.4 us
    dot_general x2, matrix products, dot_t(): lax.dot_general(a, b, (((1,), (1,)), ((), ())), preferred_element_type=F32)  12.5 us
    all_to_all x3, starting transfers between devices, send_each(): return lax.all_to_all(a, GROUP, split_axis=0, concat_axis=0, tiled=True)  11.7 us
  transfers between devices with their start and end apart: 27, of which 16 were waited for; matrix products, arithmetic and copies ran while one was open for 21% of the time, Pallas kernels for 0%

profile of v2, /device:TPU:0, one launch (start us, length us, event | category | flops | bytes accessed | tf_op | source)
XLA Modules:
  0.0 238.1 jit_solution(16999811440253773550)
XLA Ops:
  9.9 3.1 %collective-permute-start.3 = (bf16[136,2048]{1,0:T(8,128)(2,1)}, bf16[136,2048]{1,0:T(8,128)(2,1)S(1)}, u32[]{:S(2)}, u32[]{:S(2)}) collective-permute-start(bf16[136,2048]{1,0:T(8,128)(2,1)} %fusion.18), channel_id=1, source_target_pairs={{0,6},{2,0},{4,2},{6,4},{1,7},{3,1},{5,3},{7,5},{8,14},{10,8},{12,... | collective-permute-start | bytes 1671176 | tf_op jit(solution)/shard_map/ppermute | solution.py:16
  16.3 3.2 %collective-permute-start.11 = (bf16[136,2048]{1,0:T(8,128)(2,1)}, bf16[136,2048]{1,0:T(8,128)(2,1)}, u32[]{:S(2)}, u32[]{:S(2)}) collective-permute-start(bf16[136,2048]{1,0:T(8,128)(2,1)} %pad_maximum_fusion.1), channel_id=1, source_target_pairs={{0,6},{2,0},{4,2},{6,4},{1,7},{3,1},{5,3},{7,5},{8,14},{10,8},{12,... | collective-permute-start | bytes 1671176 | tf_op jit(solution)/shard_map/ppermute | solution.py:16
  19.5 6.8 %collective-permute-done.3 = bf16[136,2048]{1,0:T(8,128)(2,1)S(1)} collective-permute-done((bf16[136,2048]{1,0:T(8,128)(2,1)}, bf16[136,2048]{1,0:T(8,128)(2,1)S(1)}, u32[]{:S(2)}, u32[]{:S(2)}) %collective-permute-start.3) | collective-permute-done | bytes 557088 | tf_op jit(solution)/shard_map/ppermute | solution.py:16
  26.4 3.5 %collective-permute-done.1 = bf16[136,2048]{1,0:T(8,128)(2,1)S(1)} collective-permute-done((bf16[136,2048]{1,0:T(8,128)(2,1)}, bf16[136,2048]{1,0:T(8,128)(2,1)S(1)}, u32[]{:S(2)}, u32[]{:S(2)}) %collective-permute-start.1) | collective-permute-done | bytes 557088 | tf_op jit(solution)/shard_map/ppermute | solution.py:16
  30.1 8.2 %collective-permute-done.11 = bf16[136,2048]{1,0:T(8,128)(2,1)} collective-permute-done((bf16[136,2048]{1,0:T(8,128)(2,1)}, bf16[136,2048]{1,0:T(8,128)(2,1)}, u32[]{:S(2)}, u32[]{:S(2)}) %collective-permute-start.11) | collective-permute-done | bytes 557088 | tf_op jit(solution)/shard_map/ppermute | solution.py:16
  40.6 2.5 %collective-permute-start.14 = (bf16[72,2048]{1,0:T(8,128)(2,1)S(1)}, bf16[72,2048]{1,0:T(8,128)(2,1)S(1)}, u32[]{:S(2)}, u32[]{:S(2)}) collective-permute-start(bf16[72,2048]{1,0:T(8,128)(2,1)S(1)} %slice.233), channel_id=1, source_target_pairs={{0,6},{2,0},{4,2},{6,4},{1,7},{3,1},{5,3},{7,5},{8,14},{10,8},{12,... | collective-permute-start | bytes 884744 | tf_op jit(solution)/shard_map/ppermute | solution.py:16
  47.2 4.7 %collective-permute-done.13 = bf16[64,2048]{1,0:T(8,128)(2,1)S(1)} collective-permute-done((bf16[64,2048]{1,0:T(8,128)(2,1)S(1)}, bf16[64,2048]{1,0:T(8,128)(2,1)S(1)}, u32[]{:S(2)}, u32[]{:S(2)}) %collective-permute-start.13) | collective-permute-done | bytes 262176 | tf_op jit(solution)/shard_map/ppermute | solution.py:16
  67.9 29.4 %expert_grads.1 = (bf16[16,4608,128]{2,1,0:T(8,128)(2,1)}, bf16[512,3072]{1,0:T(8,128)(2,1)}, f32[512,1]{1,0:T(8,128)S(1)}) custom-call(bf16[2048,3072]{1,0:T(8,128)(2,1)} %bitcast.196, bf16[2048,3072]{1,0:T(8,128)(2,1)} %bitcast.197, bf16[1536,2048]{1,0:T(8,128)(2,1)} %bitcast.198, bf16[512,2048]{1,0:T(8,128)(2,1)} %fusion.9.x, ...), custom_call_target="tpu_custom_call" | custom-call | flops 25769803776 | bytes 41943040 | tf_op jit(solution)/shard_map/expert_grads/pallas_call | solution.py:118
  105.7 3.3 %all-to-all-start.1 = ((f32[8,1,64]{2,1,0:T(1,128)}), f32[8,1,64]{2,1,0:T(1,128)S(1)}, u32[]{:S(2)}, u32[]{:S(2)}) async-start(f32[8,1,64]{2,1,0:T(1,128)} %bitcast.22), calls=%async_computation.1 | async-start | bytes 8192 | tf_op jit(solution)/shard_map/all_to_all | solution.py:38
  109.0 10.7 %convolution_convert_fusion = bf16[512,2048]{1,0:T(8,128)(2,1)S(1)} fusion(bf16[512,3072]{1,0:T(8,128)(2,1)} %get-tuple-element.9, bf16[1,2048,3072]{2,1,0:T(8,128)(2,1)} %param.12), kind=kOutput, calls=%fused_computation | convolution fusion | flops 6443499520 | bytes 17825792 | tf_op jit(solution)/shard_map/dot_general | solution.py:34
  125.2 4.7 %all-to-all-start.2 = ((bf16[8,16,128]{2,1,0:T(8,128)(2,1)}), bf16[8,16,128]{2,1,0:T(8,128)(2,1)S(1)}, u32[]{:S(2)}, u32[]{:S(2)}) async-start(bf16[8,16,128]{2,1,0:T(8,128)(2,1)} %bitcast.26), calls=%async_computation.2 | async-start | bytes 65536 | tf_op jit(solution)/shard_map/all_to_all | solution.py:38
  130.6 4.7 %all-to-all-done.2 = bf16[8,16,128]{2,1,0:T(8,128)(2,1)S(1)} async-done(((bf16[8,16,128]{2,1,0:T(8,128)(2,1)}), bf16[8,16,128]{2,1,0:T(8,128)(2,1)S(1)}, u32[]{:S(2)}, u32[]{:S(2)}) %all-to-all-start.2) | async-done | bytes 32800 | tf_op jit(solution)/shard_map/all_to_all | solution.py:38
  135.5 2.9 %fusion.75 = f32[16,2048]{1,0:T(8,128)S(1)} fusion(bf16[16,1024]{1,0:T(8,128)(2,1)S(1)} %constant_dynamic-update-slice_fusion.18, bf16[1024,2048]{1,0:T(8,128)(2,1)} %slice_dynamic-update-slice_fusion), kind=kOutput, calls=%fused_computation.215 | convolution fusion | flops 67108864 | bytes 4358144 | tf_op jit(solution)/shard_map/dot_general | solution.py:264
  138.4 2.8 %collective-permute-start.18 = (f32[16,2048]{1,0:T(8,128)S(1)}, f32[16,2048]{1,0:T(8,128)S(1)}, u32[]{:S(2)}, u32[]{:S(2)}) collective-permute-start(f32[16,2048]{1,0:T(8,128)S(1)} %fusion.75), channel_id=1, source_target_pairs={{0,96},{32,0},{64,32},{96,64},{1,97},{33,1},{65,33},{97,65},{2,98}... | collective-permute-start | bytes 393224 | tf_op jit(solution)/shard_map/ppermute | solution.py:42
  143.6 4.8 %collective-permute-done.18 = f32[16,2048]{1,0:T(8,128)S(1)} collective-permute-done((f32[16,2048]{1,0:T(8,128)S(1)}, f32[16,2048]{1,0:T(8,128)S(1)}, u32[]{:S(2)}, u32[]{:S(2)}) %collective-permute-start.18) | collective-permute-done | bytes 131104 | tf_op jit(solution)/shard_map/ppermute | solution.py:42
  148.4 3.4 %collective-permute-done.17 = f32[16,2048]{1,0:T(8,128)S(1)} collective-permute-done((f32[16,2048]{1,0:T(8,128)S(1)}, f32[16,2048]{1,0:T(8,128)S(1)}, u32[]{:S(2)}, u32[]{:S(2)}) %collective-permute-start.17) | collective-permute-done | bytes 131104 | tf_op jit(solution)/shard_map/ppermute | solution.py:42
  151.8 2.3 collective-permute-done.16
  154.2 4.2 %collective-permute-start.21 = (f32[16,2048]{1,0:T(8,128)S(1)}, f32[16,2048]{1,0:T(8,128)S(1)}, u32[]{:S(2)}, u32[]{:S(2)}) collective-permute-start(f32[16,2048]{1,0:T(8,128)S(1)} %add_add_fusion.1), channel_id=1, source_target_pairs={{0,24},{8,0},{16,8},{24,16},{1,25},{9,1},{17,9},{25,17},{2,26},{10... | collective-permute-start | bytes 393224 | tf_op jit(solution)/shard_map/ppermute | solution.py:42
  160.4 3.6 %all-to-all-start = ((bf16[8,64,2048]{2,1,0:T(8,128)(2,1)}), bf16[8,64,2048]{2,1,0:T(8,128)(2,1)S(1)}, u32[]{:S(2)}, u32[]{:S(2)}) async-start(bf16[8,64,2048]{2,1,0:T(8,128)(2,1)} %dynamic-slice_dynamic-update-slice_fusion), calls=%async_computation | async-start | bytes 4194304 | tf_op jit(solution)/shard_map/all_to_all | solution.py:38
  164.0 2.9 %collective-permute-done.21 = f32[16,2048]{1,0:T(8,128)S(1)} collective-permute-done((f32[16,2048]{1,0:T(8,128)S(1)}, f32[16,2048]{1,0:T(8,128)S(1)}, u32[]{:S(2)}, u32[]{:S(2)}) %collective-permute-start.21) | collective-permute-done | bytes 131104 | tf_op jit(solution)/shard_map/ppermute | solution.py:42
  166.8 2.2 collective-permute-done.20
  170.5 28.4 %all-gather = f32[64,2048]{1,0:T(8,128)S(1)} all-gather(f32[16,2048]{1,0:T(8,128)S(1)} %add_add_fusion), channel_id=2, replica_groups=mesh['x'=4,'z'=4,'y'=4,'c'=2] {'y'}, dimensions={0}, use_global_device_ids=true | all-gather | bytes 655360 | tf_op jit(solution)/shard_map/all_gather | solution.py:266
  203.3 2.5 %copy.18 = f32[2048,128]{1,0:T(8,128)} copy(f32[2048,128]{0,1:T(8,128)} %bitcast.179) | data formatting | bytes 2097152
  208.2 20.4 %reduce-scatter.2.cloned.1.call-done = bf16[1,4608,128]{2,1,0:T(8,128)(2,1)} async-done(((bf16[1,73728,128]{2,1,0:T(8,128)(2,1)}), bf16[1,4608,128]{2,1,0:T(8,128)(2,1)}) %reduce-scatter.2.cloned.1.call-update) | async-done | bytes 1179664 | tf_op jit(solution)/shard_map/reduce_scatter | solution.py:243
  (205 shorter events, 57.6 us)
Async XLA Ops:
  7.2 221.5 %reduce-scatter.2.cloned.1.call-start = ((), (), s32[]{:S(2)}) async-start(), calls=%async_computation.4 | async-start | bytes 20054016 | tf_op jit(solution)/shard_map/reduce_scatter | solution.py:243
  9.9 16.5 %collective-permute-start.3 = (bf16[136,2048]{1,0:T(8,128)(2,1)}, bf16[136,2048]{1,0:T(8,128)(2,1)S(1)}, u32[]{:S(2)}, u32[]{:S(2)}) collective-permute-start(bf16[136,2048]{1,0:T(8,128)(2,1)} %fusion.18), channel_id=1, source_target_pairs={{0,6},{2,0},{4,2},{6,4},{1,7},{3,1},{5,3},{7,5},{8,14},{10,8},{12,... | collective-permute-start | bytes 1671176 | tf_op jit(solution)/shard_map/ppermute | solution.py:16
  13.1 16.9 %collective-permute-start.1 = (bf16[136,2048]{1,0:T(8,128)(2,1)}, bf16[136,2048]{1,0:T(8,128)(2,1)S(1)}, u32[]{:S(2)}, u32[]{:S(2)}) collective-permute-start(bf16[136,2048]{1,0:T(8,128)(2,1)} %fusion.18), channel_id=1, source_target_pairs={{0,2},{2,4},{4,6},{6,0},{1,3},{3,5},{5,7},{7,1},{8,10},{10,12},{12... | collective-permute-start | bytes 1671176 | tf_op jit(solution)/shard_map/ppermute | solution.py:16
  16.3 22.0 %collective-permute-start.11 = (bf16[136,2048]{1,0:T(8,128)(2,1)}, bf16[136,2048]{1,0:T(8,128)(2,1)}, u32[]{:S(2)}, u32[]{:S(2)}) collective-permute-start(bf16[136,2048]{1,0:T(8,128)(2,1)} %pad_maximum_fusion.1), channel_id=1, source_target_pairs={{0,6},{2,0},{4,2},{6,4},{1,7},{3,1},{5,3},{7,5},{8,14},{10,8},{12,... | collective-permute-start | bytes 1671176 | tf_op jit(solution)/shard_map/ppermute | solution.py:16
  19.5 21.1 %collective-permute-start.9 = (bf16[136,2048]{1,0:T(8,128)(2,1)}, bf16[136,2048]{1,0:T(8,128)(2,1)}, u32[]{:S(2)}, u32[]{:S(2)}) collective-permute-start(bf16[136,2048]{1,0:T(8,128)(2,1)} %pad_maximum_fusion.1), channel_id=1, source_target_pairs={{0,2},{2,4},{4,6},{6,0},{1,3},{3,5},{5,7},{7,1},{8,10},{10,12},{12... | collective-permute-start | bytes 1671176 | tf_op jit(solution)/shard_map/ppermute | solution.py:16
  19.5 24.5 %collective-permute-start = (bf16[136,2048]{1,0:T(8,128)(2,1)}, bf16[136,2048]{1,0:T(8,128)(2,1)S(1)}, u32[]{:S(2)}, u32[]{:S(2)}) collective-permute-start(bf16[136,2048]{1,0:T(8,128)(2,1)} %fusion.18), channel_id=1, source_target_pairs={{0,1},{1,0},{2,3},{3,2},{4,5},{5,4},{6,7},{7,6},{8,9},{9,8},{10,11... | collective-permute-start | bytes 1671176 | tf_op jit(solution)/shard_map/ppermute | solution.py:20
  26.4 17.8 %collective-permute-start.8 = (bf16[136,2048]{1,0:T(8,128)(2,1)}, bf16[136,2048]{1,0:T(8,128)(2,1)S(1)}, u32[]{:S(2)}, u32[]{:S(2)}) collective-permute-start(bf16[136,2048]{1,0:T(8,128)(2,1)} %pad_maximum_fusion.1), channel_id=1, source_target_pairs={{0,1},{1,0},{2,3},{3,2},{4,5},{5,4},{6,7},{7,6},{8,9},{9,8},{10,11... | collective-permute-start | bytes 1671176 | tf_op jit(solution)/shard_map/ppermute | solution.py:20
  30.0 22.0 %collective-permute-start.5 = (bf16[72,2048]{1,0:T(8,128)(2,1)S(1)}, bf16[72,2048]{1,0:T(8,128)(2,1)S(1)}, u32[]{:S(2)}, u32[]{:S(2)}) collective-permute-start(bf16[72,2048]{1,0:T(8,128)(2,1)S(1)} %slice.218), channel_id=1, source_target_pairs={{0,6},{2,0},{4,2},{6,4},{1,7},{3,1},{5,3},{7,5},{8,14},{10,8},{12,... | collective-permute-start | bytes 884744 | tf_op jit(solution)/shard_map/ppermute | solution.py:16
  38.3 8.9 %collective-permute-start.6 = (bf16[64,2048]{1,0:T(8,128)(2,1)S(1)}, bf16[64,2048]{1,0:T(8,128)(2,1)S(1)}, u32[]{:S(2)}, u32[]{:S(2)}) collective-permute-start(bf16[64,2048]{1,0:T(8,128)(2,1)S(1)} %slice.220), channel_id=1, source_target_pairs={{0,2},{2,4},{4,6},{6,0},{1,3},{3,5},{5,7},{7,1},{8,10},{10,12},{12... | collective-permute-start | bytes 786440 | tf_op jit(solution)/shard_map/ppermute | solution.py:16
  40.6 12.0 %collective-permute-start.14 = (bf16[72,2048]{1,0:T(8,128)(2,1)S(1)}, bf16[72,2048]{1,0:T(8,128)(2,1)S(1)}, u32[]{:S(2)}, u32[]{:S(2)}) collective-permute-start(bf16[72,2048]{1,0:T(8,128)(2,1)S(1)} %slice.233), channel_id=1, source_target_pairs={{0,6},{2,0},{4,2},{6,4},{1,7},{3,1},{5,3},{7,5},{8,14},{10,8},{12,... | collective-permute-start | bytes 884744 | tf_op jit(solution)/shard_map/ppermute | solution.py:16
  44.1 7.9 %collective-permute-start.13 = (bf16[64,2048]{1,0:T(8,128)(2,1)S(1)}, bf16[64,2048]{1,0:T(8,128)(2,1)S(1)}, u32[]{:S(2)}, u32[]{:S(2)}) collective-permute-start(bf16[64,2048]{1,0:T(8,128)(2,1)S(1)} %slice.232), channel_id=1, source_target_pairs={{0,2},{2,4},{4,6},{6,0},{1,3},{3,5},{5,7},{7,1},{8,10},{10,12},{12... | collective-permute-start | bytes 786440 | tf_op jit(solution)/shard_map/ppermute | solution.py:16
  45.1 8.5 %collective-permute-start.4 = (bf16[136,2048]{1,0:T(8,128)(2,1)S(1)}, bf16[136,2048]{1,0:T(8,128)(2,1)S(1)}, u32[]{:S(2)}, u32[]{:S(2)}) collective-permute-start(bf16[136,2048]{1,0:T(8,128)(2,1)S(1)} %collective-permute-done.3), channel_id=1, source_target_pairs={{0,1},{1,0},{2,3},{3,2},{4,5},{5,4},{6,7},{7,6},{8,9},{9,8},{10,11... | collective-permute-start | bytes 1671176 | tf_op jit(solution)/shard_map/ppermute | solution.py:20
  47.2 5.6 %collective-permute-start.2 = (bf16[136,2048]{1,0:T(8,128)(2,1)S(1)}, bf16[136,2048]{1,0:T(8,128)(2,1)S(1)}, u32[]{:S(2)}, u32[]{:S(2)}) collective-permute-start(bf16[136,2048]{1,0:T(8,128)(2,1)S(1)} %collective-permute-done.1), channel_id=1, source_target_pairs={{0,1},{1,0},{2,3},{3,2},{4,5},{5,4},{6,7},{7,6},{8,9},{9,8},{10,11... | collective-permute-start | bytes 1671176 | tf_op jit(solution)/shard_map/ppermute | solution.py:20
  52.7 7.3 %collective-permute-start.7 = (bf16[136,2048]{1,0:T(8,128)(2,1)S(1)}, bf16[136,2048]{1,0:T(8,128)(2,1)S(1)}, u32[]{:S(2)}, u32[]{:S(2)}) collective-permute-start(bf16[136,2048]{1,0:T(8,128)(2,1)S(1)} %constant_dynamic-update-slice_fusion.6), channel_id=1, source_target_pairs={{0,1},{1,0},{2,3},{3,2},{4,5},{5,4},{6,7},{7,6},{8,9},{9,8},{10,11... | collective-permute-start | bytes 1671176 | tf_op jit(solution)/shard_map/ppermute | solution.py:20
  52.8 7.4 %collective-permute-start.15 = (bf16[136,2048]{1,0:T(8,128)(2,1)S(1)}, bf16[136,2048]{1,0:T(8,128)(2,1)S(1)}, u32[]{:S(2)}, u32[]{:S(2)}) collective-permute-start(bf16[136,2048]{1,0:T(8,128)(2,1)S(1)} %constant_dynamic-update-slice_fusion.8), channel_id=1, source_target_pairs={{0,1},{1,0},{2,3},{3,2},{4,5},{5,4},{6,7},{7,6},{8,9},{9,8},{10,11... | collective-permute-start | bytes 1671176 | tf_op jit(solution)/shard_map/ppermute | solution.py:20
  105.7 18.6 %all-to-all-start.1 = ((f32[8,1,64]{2,1,0:T(1,128)}), f32[8,1,64]{2,1,0:T(1,128)S(1)}, u32[]{:S(2)}, u32[]{:S(2)}) async-start(f32[8,1,64]{2,1,0:T(1,128)} %bitcast.22), calls=%async_computation.1 | async-start | bytes 8192 | tf_op jit(solution)/shard_map/all_to_all | solution.py:38
  125.2 10.2 %all-to-all-start.2 = ((bf16[8,16,128]{2,1,0:T(8,128)(2,1)}), bf16[8,16,128]{2,1,0:T(8,128)(2,1)S(1)}, u32[]{:S(2)}, u32[]{:S(2)}) async-start(bf16[8,16,128]{2,1,0:T(8,128)(2,1)} %bitcast.26), calls=%async_computation.2 | async-start | bytes 65536 | tf_op jit(solution)/shard_map/all_to_all | solution.py:38
  138.4 10.0 %collective-permute-start.18 = (f32[16,2048]{1,0:T(8,128)S(1)}, f32[16,2048]{1,0:T(8,128)S(1)}, u32[]{:S(2)}, u32[]{:S(2)}) collective-permute-start(f32[16,2048]{1,0:T(8,128)S(1)} %fusion.75), channel_id=1, source_target_pairs={{0,96},{32,0},{64,32},{96,64},{1,97},{33,1},{65,33},{97,65},{2,98}... | collective-permute-start | bytes 393224 | tf_op jit(solution)/shard_map/ppermute | solution.py:42
  141.1 10.7 %collective-permute-start.17 = (f32[16,2048]{1,0:T(8,128)S(1)}, f32[16,2048]{1,0:T(8,128)S(1)}, u32[]{:S(2)}, u32[]{:S(2)}) collective-permute-start(f32[16,2048]{1,0:T(8,128)S(1)} %fusion.75), channel_id=1, source_target_pairs={{0,64},{32,96},{64,0},{96,32},{1,65},{33,97},{65,1},{97,33},{2,66}... | collective-permute-start | bytes 393224 | tf_op jit(solution)/shard_map/ppermute | solution.py:42
  141.9 12.2 %collective-permute-start.16 = (f32[16,2048]{1,0:T(8,128)S(1)}, f32[16,2048]{1,0:T(8,128)S(1)}, u32[]{:S(2)}, u32[]{:S(2)}) collective-permute-start(f32[16,2048]{1,0:T(8,128)S(1)} %fusion.75), channel_id=1, source_target_pairs={{0,32},{32,64},{64,96},{96,0},{1,33},{33,65},{65,97},{97,1},{2,34}... | collective-permute-start | bytes 393224 | tf_op jit(solution)/shard_map/ppermute | solution.py:42
  154.2 12.7 %collective-permute-start.21 = (f32[16,2048]{1,0:T(8,128)S(1)}, f32[16,2048]{1,0:T(8,128)S(1)}, u32[]{:S(2)}, u32[]{:S(2)}) collective-permute-start(f32[16,2048]{1,0:T(8,128)S(1)} %add_add_fusion.1), channel_id=1, source_target_pairs={{0,24},{8,0},{16,8},{24,16},{1,25},{9,1},{17,9},{25,17},{2,26},{10... | collective-permute-start | bytes 393224 | tf_op jit(solution)/shard_map/ppermute | solution.py:42
  158.4 10.7 %collective-permute-start.20 = (f32[16,2048]{1,0:T(8,128)S(1)}, f32[16,2048]{1,0:T(8,128)S(1)}, u32[]{:S(2)}, u32[]{:S(2)}) collective-permute-start(f32[16,2048]{1,0:T(8,128)S(1)} %add_add_fusion.1), channel_id=1, source_target_pairs={{0,16},{8,24},{16,0},{24,8},{1,17},{9,25},{17,1},{25,9},{2,18},{10... | collective-permute-start | bytes 393224 | tf_op jit(solution)/shard_map/ppermute | solution.py:42
  158.4 12.1 %collective-permute-start.19 = (f32[16,2048]{1,0:T(8,128)S(1)}, f32[16,2048]{1,0:T(8,128)S(1)}, u32[]{:S(2)}, u32[]{:S(2)}) collective-permute-start(f32[16,2048]{1,0:T(8,128)S(1)} %add_add_fusion.1), channel_id=1, source_target_pairs={{0,8},{8,16},{16,24},{24,0},{1,9},{9,17},{17,25},{25,1},{2,10},{10... | collective-permute-start | bytes 393224 | tf_op jit(solution)/shard_map/ppermute | solution.py:42
  160.4 45.5 %all-to-all-start = ((bf16[8,64,2048]{2,1,0:T(8,128)(2,1)}), bf16[8,64,2048]{2,1,0:T(8,128)(2,1)S(1)}, u32[]{:S(2)}, u32[]{:S(2)}) async-start(bf16[8,64,2048]{2,1,0:T(8,128)(2,1)} %dynamic-slice_dynamic-update-slice_fusion), calls=%async_computation | async-start | bytes 4194304 | tf_op jit(solution)/shard_map/all_to_all | solution.py:38
  (29 other events, 184.1 us)
Sparse Core Ops, SparseCore 0:
  97.5 131.1 reduce-scatter.1

commit v3 on v2

--- a/solution.py
+++ b/solution.py
@@ -39,8 +39,11 @@
 
 
 def ring_all(a, axis):
-    others = [lax.ppermute(a, axis, [(i, (i + k) % 4) for i in range(4)]) for k in (1, 2, 3)]
-    return a + others[0] + others[1] + others[2]
+    sent = a.astype(BF)
+    near, far, last = (
+        lax.ppermute(sent, axis, [(i, (i + k) % 4) for i in range(4)]).astype(F32) for k in (1, 2, 3)
+    )
+    return (sent.astype(F32) + far) + (near + last)
 
 
 LANES = 128
@@ -167,7 +170,7 @@
         ],
         compiler_params=pltpu.CompilerParams(vmem_limit_bytes=8 * 2**20),
         name="unpack",
-    )(total)
+    )(in_hbm(total))
 
 
 def step(tokens, out_grad, z_weight, router_weight, expert_ids, gate_up_weight, down_weight):

time: 239 us -> 234 us (0.979)
  waiting for transfers between devices: 70.2 us -> 58.6 us
  blocking collectives: 28.4 us -> 33.4 us
    ppermute x6, waiting for transfers between devices: 17.1 us -> 7.54 us  [ring_all(): lax.ppermute(sent, axis, [(i, (i + k) % 4) for i in range(4)]).astype(F32)]
    all_gather x1, blocking collectives: 28.4 us -> 33.4 us  [step(): near = lax.all_gather(router_part, 'y', axis=0, tiled=False)]
    unnamed x87 -> x85, local copies, waits for them, and re-layouts: 16.4 us -> 15.2 us
  transfers between devices with their start and end apart: 27 -> 27, of which waited for: 16 -> 15; matrix products, arithmetic and copies ran while one was open for 21% -> 21% of each run, Pallas kernels for 0% -> 0%
where the time goes in v3:
time: 234 us; the launch traced here: 233 us
  waiting for transfers between devices  58.6 us (25%)
  starting transfers between devices  34.6 us (15%)
  blocking collectives  33.4 us (14%)
  Pallas kernels  32 us (14%)
  matrix products  29 us (12%)
  local copies, waits for them, and re-layouts  22.5 us (10%)
  between operations  14.9 us (6%)
  other arithmetic  7.93 us (3%)
    all_gather x1, blocking collectives, step(): near = lax.all_gather(router_part, 'y', axis=0, tiled=False)  33.4 us
    pallas_call x1, Pallas kernels, expert_grads(): pl.pallas_call(expert_kernel, grid=(TILES + 4,), in_specs=[pl.BlockSpec((...  29.4 us
    ppermute x8, waiting for transfers between devices, shift(): return lax.ppermute(a, 'y', [(i, (i + step) % 4) for i in range(4)])  24.8 us
    reduce_scatter x1, waiting for transfers between devices, step(): lax.psum_scatter(parts.reshape(1, -1, parts.shape[2]), DP, scatter_dimens...  18.4 us
    unnamed x85, local copies, waits for them, and re-layouts  15.2 us
    dot_general x2, matrix products, dot_t(): lax.dot_general(a, b, (((1,), (1,)), ((), ())), preferred_element_type=F32)  12.5 us
    all_to_all x3, starting transfers between devices, send_each(): return lax.all_to_all(a, GROUP, split_axis=0, concat_axis=0, tiled=True)  11.7 us
    ppermute x6, starting transfers between devices, ring_all(): lax.ppermute(sent, axis, [(i, (i + k) % 4) for i in range(4)]).astype(F32)  11.2 us
  transfers between devices with their start and end apart: 27, of which 15 were waited for; matrix products, arithmetic and copies ran while one was open for 21% of the time, Pallas kernels for 0%

profile of v3, /device:TPU:0, one launch (start us, length us, event | category | flops | bytes accessed | tf_op | source)
XLA Modules:
  0.0 232.8 jit_solution(8872793046834132589)
XLA Ops:
  9.9 3.1 %collective-permute-start.3 = (bf16[136,2048]{1,0:T(8,128)(2,1)}, bf16[136,2048]{1,0:T(8,128)(2,1)S(1)}, u32[]{:S(2)}, u32[]{:S(2)}) collective-permute-start(bf16[136,2048]{1,0:T(8,128)(2,1)} %fusion.18), channel_id=1, source_target_pairs={{0,6},{2,0},{4,2},{6,4},{1,7},{3,1},{5,3},{7,5},{8,14},{10,8},{12,... | collective-permute-start | bytes 1671176 | tf_op jit(solution)/shard_map/ppermute | solution.py:16
  16.3 3.2 %collective-permute-start.11 = (bf16[136,2048]{1,0:T(8,128)(2,1)}, bf16[136,2048]{1,0:T(8,128)(2,1)}, u32[]{:S(2)}, u32[]{:S(2)}) collective-permute-start(bf16[136,2048]{1,0:T(8,128)(2,1)} %pad_maximum_fusion.1), channel_id=1, source_target_pairs={{0,6},{2,0},{4,2},{6,4},{1,7},{3,1},{5,3},{7,5},{8,14},{10,8},{12,... | collective-permute-start | bytes 1671176 | tf_op jit(solution)/shard_map/ppermute | solution.py:16
  19.5 6.8 %collective-permute-done.3 = bf16[136,2048]{1,0:T(8,128)(2,1)S(1)} collective-permute-done((bf16[136,2048]{1,0:T(8,128)(2,1)}, bf16[136,2048]{1,0:T(8,128)(2,1)S(1)}, u32[]{:S(2)}, u32[]{:S(2)}) %collective-permute-start.3) | collective-permute-done | bytes 557088 | tf_op jit(solution)/shard_map/ppermute | solution.py:16
  26.4 3.5 %collective-permute-done.1 = bf16[136,2048]{1,0:T(8,128)(2,1)S(1)} collective-permute-done((bf16[136,2048]{1,0:T(8,128)(2,1)}, bf16[136,2048]{1,0:T(8,128)(2,1)S(1)}, u32[]{:S(2)}, u32[]{:S(2)}) %collective-permute-start.1) | collective-permute-done | bytes 557088 | tf_op jit(solution)/shard_map/ppermute | solution.py:16
  30.1 8.2 %collective-permute-done.11 = bf16[136,2048]{1,0:T(8,128)(2,1)} collective-permute-done((bf16[136,2048]{1,0:T(8,128)(2,1)}, bf16[136,2048]{1,0:T(8,128)(2,1)}, u32[]{:S(2)}, u32[]{:S(2)}) %collective-permute-start.11) | collective-permute-done | bytes 557088 | tf_op jit(solution)/shard_map/ppermute | solution.py:16
  40.6 2.5 %collective-permute-start.14 = (bf16[72,2048]{1,0:T(8,128)(2,1)S(1)}, bf16[72,2048]{1,0:T(8,128)(2,1)S(1)}, u32[]{:S(2)}, u32[]{:S(2)}) collective-permute-start(bf16[72,2048]{1,0:T(8,128)(2,1)S(1)} %slice.233), channel_id=1, source_target_pairs={{0,6},{2,0},{4,2},{6,4},{1,7},{3,1},{5,3},{7,5},{8,14},{10,8},{12,... | collective-permute-start | bytes 884744 | tf_op jit(solution)/shard_map/ppermute | solution.py:16
  47.2 4.7 %collective-permute-done.13 = bf16[64,2048]{1,0:T(8,128)(2,1)S(1)} collective-permute-done((bf16[64,2048]{1,0:T(8,128)(2,1)S(1)}, bf16[64,2048]{1,0:T(8,128)(2,1)S(1)}, u32[]{:S(2)}, u32[]{:S(2)}) %collective-permute-start.13) | collective-permute-done | bytes 262176 | tf_op jit(solution)/shard_map/ppermute | solution.py:16
  62.0 2.0 fusion.2
  67.9 29.4 %expert_grads.1 = (bf16[16,4608,128]{2,1,0:T(8,128)(2,1)}, bf16[512,3072]{1,0:T(8,128)(2,1)}, f32[512,1]{1,0:T(8,128)S(1)}) custom-call(bf16[2048,3072]{1,0:T(8,128)(2,1)} %bitcast.196, bf16[2048,3072]{1,0:T(8,128)(2,1)} %bitcast.197, bf16[1536,2048]{1,0:T(8,128)(2,1)} %bitcast.198, bf16[512,2048]{1,0:T(8,128)(2,1)} %fusion.9.x, ...), custom_call_target="tpu_custom_call" | custom-call | flops 25769803776 | bytes 41943040 | tf_op jit(solution)/shard_map/expert_grads/pallas_call | solution.py:121
  105.7 3.3 %all-to-all-start.1 = ((f32[8,1,64]{2,1,0:T(1,128)}), f32[8,1,64]{2,1,0:T(1,128)S(1)}, u32[]{:S(2)}, u32[]{:S(2)}) async-start(f32[8,1,64]{2,1,0:T(1,128)} %bitcast.22), calls=%async_computation.1 | async-start | bytes 8192 | tf_op jit(solution)/shard_map/all_to_all | solution.py:38
  109.0 10.7 %convolution_convert_fusion = bf16[512,2048]{1,0:T(8,128)(2,1)S(1)} fusion(bf16[512,3072]{1,0:T(8,128)(2,1)} %get-tuple-element.9, bf16[1,2048,3072]{2,1,0:T(8,128)(2,1)} %param.12), kind=kOutput, calls=%fused_computation | convolution fusion | flops 6443499520 | bytes 17825792 | tf_op jit(solution)/shard_map/dot_general | solution.py:34
  125.2 4.7 %all-to-all-start.2 = ((bf16[8,16,128]{2,1,0:T(8,128)(2,1)}), bf16[8,16,128]{2,1,0:T(8,128)(2,1)S(1)}, u32[]{:S(2)}, u32[]{:S(2)}) async-start(bf16[8,16,128]{2,1,0:T(8,128)(2,1)} %bitcast.26), calls=%async_computation.2 | async-start | bytes 65536 | tf_op jit(solution)/shard_map/all_to_all | solution.py:38
  130.6 4.7 %all-to-all-done.2 = bf16[8,16,128]{2,1,0:T(8,128)(2,1)S(1)} async-done(((bf16[8,16,128]{2,1,0:T(8,128)(2,1)}), bf16[8,16,128]{2,1,0:T(8,128)(2,1)S(1)}, u32[]{:S(2)}, u32[]{:S(2)}) %all-to-all-start.2) | async-done | bytes 32800 | tf_op jit(solution)/shard_map/all_to_all | solution.py:38
  135.5 2.9 %convolution_convert_fusion.17 = bf16[16,2048]{1,0:T(8,128)(2,1)S(1)} fusion(bf16[16,1024]{1,0:T(8,128)(2,1)S(1)} %constant_dynamic-update-slice_fusion.18, bf16[1024,2048]{1,0:T(8,128)(2,1)} %slice_dynamic-update-slice_fusion), kind=kOutput, calls=%fused_computation.36 | convolution fusion | flops 67141632 | bytes 4292608 | tf_op jit(solution)/shard_map/dot_general | solution.py:267
  138.4 2.8 %collective-permute-start.18 = (bf16[16,2048]{1,0:T(8,128)(2,1)S(1)}, bf16[16,2048]{1,0:T(8,128)(2,1)S(1)}, u32[]{:S(2)}, u32[]{:S(2)}) collective-permute-start(bf16[16,2048]{1,0:T(8,128)(2,1)S(1)} %convolution_convert_fusion.17), channel_id=1, source_target_pairs={{0,96},{32,0},{64,32},{96,64},{1,97},{33,1},{65,33},{97,65},{2,98}... | collective-permute-start | bytes 196616 | tf_op jit(solution)/shard_map/ppermute | solution.py:44
  141.1 2.3 %collective-permute-start.16 = (bf16[16,2048]{1,0:T(8,128)(2,1)S(1)}, bf16[16,2048]{1,0:T(8,128)(2,1)S(1)}, u32[]{:S(2)}, u32[]{:S(2)}) collective-permute-start(bf16[16,2048]{1,0:T(8,128)(2,1)S(1)} %convolution_convert_fusion.17), channel_id=1, source_target_pairs={{0,64},{32,96},{64,0},{96,32},{1,65},{33,97},{65,1},{97,33},{2,66}... | collective-permute-start | bytes 196616 | tf_op jit(solution)/shard_map/ppermute | solution.py:44
  144.6 4.9 %collective-permute-done.17 = bf16[16,2048]{1,0:T(8,128)(2,1)S(1)} collective-permute-done((bf16[16,2048]{1,0:T(8,128)(2,1)S(1)}, bf16[16,2048]{1,0:T(8,128)(2,1)S(1)}, u32[]{:S(2)}, u32[]{:S(2)}) %collective-permute-start.17) | collective-permute-done | bytes 65568 | tf_op jit(solution)/shard_map/ppermute | solution.py:44
  150.2 4.3 %collective-permute-start.21 = (bf16[16,2048]{1,0:T(8,128)(2,1)S(1)}, bf16[16,2048]{1,0:T(8,128)(2,1)S(1)}, u32[]{:S(2)}, u32[]{:S(2)}) collective-permute-start(bf16[16,2048]{1,0:T(8,128)(2,1)S(1)} %add_convert_fusion), channel_id=1, source_target_pairs={{0,24},{8,0},{16,8},{24,16},{1,25},{9,1},{17,9},{25,17},{2,26},{10... | collective-permute-start | bytes 196616 | tf_op jit(solution)/shard_map/ppermute | solution.py:44
  157.0 3.6 %all-to-all-start = ((bf16[8,64,2048]{2,1,0:T(8,128)(2,1)}), bf16[8,64,2048]{2,1,0:T(8,128)(2,1)S(1)}, u32[]{:S(2)}, u32[]{:S(2)}) async-start(bf16[8,64,2048]{2,1,0:T(8,128)(2,1)} %dynamic-slice_dynamic-update-slice_fusion), calls=%async_computation | async-start | bytes 4194304 | tf_op jit(solution)/shard_map/all_to_all | solution.py:38
  162.3 33.4 %all-gather = f32[64,2048]{1,0:T(8,128)S(1)} all-gather(f32[16,2048]{1,0:T(8,128)S(1)} %add_add_fusion), channel_id=2, replica_groups=mesh['x'=4,'z'=4,'y'=4,'c'=2] {'y'}, dimensions={0}, use_global_device_ids=true | all-gather | bytes 655360 | tf_op jit(solution)/shard_map/all_gather | solution.py:269
  195.7 2.0 collective-permute-done.22
  200.0 2.6 %copy.18 = f32[2048,128]{1,0:T(8,128)} copy(f32[2048,128]{0,1:T(8,128)} %bitcast.178) | data formatting | bytes 2097152
  205.0 18.4 %reduce-scatter.2.cloned.1.call-done = bf16[1,4608,128]{2,1,0:T(8,128)(2,1)} async-done(((bf16[1,73728,128]{2,1,0:T(8,128)(2,1)}), bf16[1,4608,128]{2,1,0:T(8,128)(2,1)}) %reduce-scatter.2.cloned.1.call-update) | async-done | bytes 1179664 | tf_op jit(solution)/shard_map/reduce_scatter | solution.py:246
  223.4 2.6 %unpack.1 = (bf16[128,3072]{1,0:T(8,128)(2,1)}, bf16[96,2048]{1,0:T(8,128)(2,1)}) custom-call(bf16[4608,128]{1,0:T(8,128)(2,1)} %bitcast.189), custom_call_target="tpu_custom_call" | custom-call | tf_op jit(solution)/shard_map/unpack/pallas_call | solution.py:165
  (203 shorter events, 51.1 us)
Async XLA Ops:
  7.2 216.2 %reduce-scatter.2.cloned.1.call-start = ((), (), s32[]{:S(2)}) async-start(), calls=%async_computation.4 | async-start | bytes 20054016 | tf_op jit(solution)/shard_map/reduce_scatter | solution.py:246
  9.9 16.5 %collective-permute-start.3 = (bf16[136,2048]{1,0:T(8,128)(2,1)}, bf16[136,2048]{1,0:T(8,128)(2,1)S(1)}, u32[]{:S(2)}, u32[]{:S(2)}) collective-permute-start(bf16[136,2048]{1,0:T(8,128)(2,1)} %fusion.18), channel_id=1, source_target_pairs={{0,6},{2,0},{4,2},{6,4},{1,7},{3,1},{5,3},{7,5},{8,14},{10,8},{12,... | collective-permute-start | bytes 1671176 | tf_op jit(solution)/shard_map/ppermute | solution.py:16
  13.1 16.9 %collective-permute-start.1 = (bf16[136,2048]{1,0:T(8,128)(2,1)}, bf16[136,2048]{1,0:T(8,128)(2,1)S(1)}, u32[]{:S(2)}, u32[]{:S(2)}) collective-permute-start(bf16[136,2048]{1,0:T(8,128)(2,1)} %fusion.18), channel_id=1, source_target_pairs={{0,2},{2,4},{4,6},{6,0},{1,3},{3,5},{5,7},{7,1},{8,10},{10,12},{12... | collective-permute-start | bytes 1671176 | tf_op jit(solution)/shard_map/ppermute | solution.py:16
  16.3 22.0 %collective-permute-start.11 = (bf16[136,2048]{1,0:T(8,128)(2,1)}, bf16[136,2048]{1,0:T(8,128)(2,1)}, u32[]{:S(2)}, u32[]{:S(2)}) collective-permute-start(bf16[136,2048]{1,0:T(8,128)(2,1)} %pad_maximum_fusion.1), channel_id=1, source_target_pairs={{0,6},{2,0},{4,2},{6,4},{1,7},{3,1},{5,3},{7,5},{8,14},{10,8},{12,... | collective-permute-start | bytes 1671176 | tf_op jit(solution)/shard_map/ppermute | solution.py:16
  19.5 21.1 %collective-permute-start.9 = (bf16[136,2048]{1,0:T(8,128)(2,1)}, bf16[136,2048]{1,0:T(8,128)(2,1)}, u32[]{:S(2)}, u32[]{:S(2)}) collective-permute-start(bf16[136,2048]{1,0:T(8,128)(2,1)} %pad_maximum_fusion.1), channel_id=1, source_target_pairs={{0,2},{2,4},{4,6},{6,0},{1,3},{3,5},{5,7},{7,1},{8,10},{10,12},{12... | collective-permute-start | bytes 1671176 | tf_op jit(solution)/shard_map/ppermute | solution.py:16
  19.5 24.5 %collective-permute-start = (bf16[136,2048]{1,0:T(8,128)(2,1)}, bf16[136,2048]{1,0:T(8,128)(2,1)S(1)}, u32[]{:S(2)}, u32[]{:S(2)}) collective-permute-start(bf16[136,2048]{1,0:T(8,128)(2,1)} %fusion.18), channel_id=1, source_target_pairs={{0,1},{1,0},{2,3},{3,2},{4,5},{5,4},{6,7},{7,6},{8,9},{9,8},{10,11... | collective-permute-start | bytes 1671176 | tf_op jit(solution)/shard_map/ppermute | solution.py:20
  26.4 17.8 %collective-permute-start.8 = (bf16[136,2048]{1,0:T(8,128)(2,1)}, bf16[136,2048]{1,0:T(8,128)(2,1)S(1)}, u32[]{:S(2)}, u32[]{:S(2)}) collective-permute-start(bf16[136,2048]{1,0:T(8,128)(2,1)} %pad_maximum_fusion.1), channel_id=1, source_target_pairs={{0,1},{1,0},{2,3},{3,2},{4,5},{5,4},{6,7},{7,6},{8,9},{9,8},{10,11... | collective-permute-start | bytes 1671176 | tf_op jit(solution)/shard_map/ppermute | solution.py:20
  30.0 22.0 %collective-permute-start.5 = (bf16[72,2048]{1,0:T(8,128)(2,1)S(1)}, bf16[72,2048]{1,0:T(8,128)(2,1)S(1)}, u32[]{:S(2)}, u32[]{:S(2)}) collective-permute-start(bf16[72,2048]{1,0:T(8,128)(2,1)S(1)} %slice.218), channel_id=1, source_target_pairs={{0,6},{2,0},{4,2},{6,4},{1,7},{3,1},{5,3},{7,5},{8,14},{10,8},{12,... | collective-permute-start | bytes 884744 | tf_op jit(solution)/shard_map/ppermute | solution.py:16
  38.3 8.9 %collective-permute-start.6 = (bf16[64,2048]{1,0:T(8,128)(2,1)S(1)}, bf16[64,2048]{1,0:T(8,128)(2,1)S(1)}, u32[]{:S(2)}, u32[]{:S(2)}) collective-permute-start(bf16[64,2048]{1,0:T(8,128)(2,1)S(1)} %slice.220), channel_id=1, source_target_pairs={{0,2},{2,4},{4,6},{6,0},{1,3},{3,5},{5,7},{7,1},{8,10},{10,12},{12... | collective-permute-start | bytes 786440 | tf_op jit(solution)/shard_map/ppermute | solution.py:16
  40.6 12.0 %collective-permute-start.14 = (bf16[72,2048]{1,0:T(8,128)(2,1)S(1)}, bf16[72,2048]{1,0:T(8,128)(2,1)S(1)}, u32[]{:S(2)}, u32[]{:S(2)}) collective-permute-start(bf16[72,2048]{1,0:T(8,128)(2,1)S(1)} %slice.233), channel_id=1, source_target_pairs={{0,6},{2,0},{4,2},{6,4},{1,7},{3,1},{5,3},{7,5},{8,14},{10,8},{12,... | collective-permute-start | bytes 884744 | tf_op jit(solution)/shard_map/ppermute | solution.py:16
  44.1 7.9 %collective-permute-start.13 = (bf16[64,2048]{1,0:T(8,128)(2,1)S(1)}, bf16[64,2048]{1,0:T(8,128)(2,1)S(1)}, u32[]{:S(2)}, u32[]{:S(2)}) collective-permute-start(bf16[64,2048]{1,0:T(8,128)(2,1)S(1)} %slice.232), channel_id=1, source_target_pairs={{0,2},{2,4},{4,6},{6,0},{1,3},{3,5},{5,7},{7,1},{8,10},{10,12},{12... | collective-permute-start | bytes 786440 | tf_op jit(solution)/shard_map/ppermute | solution.py:16
  45.1 8.5 %collective-permute-start.4 = (bf16[136,2048]{1,0:T(8,128)(2,1)S(1)}, bf16[136,2048]{1,0:T(8,128)(2,1)S(1)}, u32[]{:S(2)}, u32[]{:S(2)}) collective-permute-start(bf16[136,2048]{1,0:T(8,128)(2,1)S(1)} %collective-permute-done.3), channel_id=1, source_target_pairs={{0,1},{1,0},{2,3},{3,2},{4,5},{5,4},{6,7},{7,6},{8,9},{9,8},{10,11... | collective-permute-start | bytes 1671176 | tf_op jit(solution)/shard_map/ppermute | solution.py:20
  47.2 5.6 %collective-permute-start.2 = (bf16[136,2048]{1,0:T(8,128)(2,1)S(1)}, bf16[136,2048]{1,0:T(8,128)(2,1)S(1)}, u32[]{:S(2)}, u32[]{:S(2)}) collective-permute-start(bf16[136,2048]{1,0:T(8,128)(2,1)S(1)} %collective-permute-done.1), channel_id=1, source_target_pairs={{0,1},{1,0},{2,3},{3,2},{4,5},{5,4},{6,7},{7,6},{8,9},{9,8},{10,11... | collective-permute-start | bytes 1671176 | tf_op jit(solution)/shard_map/ppermute | solution.py:20
  52.7 7.3 %collective-permute-start.7 = (bf16[136,2048]{1,0:T(8,128)(2,1)S(1)}, bf16[136,2048]{1,0:T(8,128)(2,1)S(1)}, u32[]{:S(2)}, u32[]{:S(2)}) collective-permute-start(bf16[136,2048]{1,0:T(8,128)(2,1)S(1)} %constant_dynamic-update-slice_fusion.6), channel_id=1, source_target_pairs={{0,1},{1,0},{2,3},{3,2},{4,5},{5,4},{6,7},{7,6},{8,9},{9,8},{10,11... | collective-permute-start | bytes 1671176 | tf_op jit(solution)/shard_map/ppermute | solution.py:20
  52.8 7.4 %collective-permute-start.15 = (bf16[136,2048]{1,0:T(8,128)(2,1)S(1)}, bf16[136,2048]{1,0:T(8,128)(2,1)S(1)}, u32[]{:S(2)}, u32[]{:S(2)}) collective-permute-start(bf16[136,2048]{1,0:T(8,128)(2,1)S(1)} %constant_dynamic-update-slice_fusion.8), channel_id=1, source_target_pairs={{0,1},{1,0},{2,3},{3,2},{4,5},{5,4},{6,7},{7,6},{8,9},{9,8},{10,11... | collective-permute-start | bytes 1671176 | tf_op jit(solution)/shard_map/ppermute | solution.py:20
  105.7 18.6 %all-to-all-start.1 = ((f32[8,1,64]{2,1,0:T(1,128)}), f32[8,1,64]{2,1,0:T(1,128)S(1)}, u32[]{:S(2)}, u32[]{:S(2)}) async-start(f32[8,1,64]{2,1,0:T(1,128)} %bitcast.22), calls=%async_computation.1 | async-start | bytes 8192 | tf_op jit(solution)/shard_map/all_to_all | solution.py:38
  125.2 10.2 %all-to-all-start.2 = ((bf16[8,16,128]{2,1,0:T(8,128)(2,1)}), bf16[8,16,128]{2,1,0:T(8,128)(2,1)S(1)}, u32[]{:S(2)}, u32[]{:S(2)}) async-start(bf16[8,16,128]{2,1,0:T(8,128)(2,1)} %bitcast.26), calls=%async_computation.2 | async-start | bytes 65536 | tf_op jit(solution)/shard_map/all_to_all | solution.py:38
  138.4 6.2 %collective-permute-start.18 = (bf16[16,2048]{1,0:T(8,128)(2,1)S(1)}, bf16[16,2048]{1,0:T(8,128)(2,1)S(1)}, u32[]{:S(2)}, u32[]{:S(2)}) collective-permute-start(bf16[16,2048]{1,0:T(8,128)(2,1)S(1)} %convolution_convert_fusion.17), channel_id=1, source_target_pairs={{0,96},{32,0},{64,32},{96,64},{1,97},{33,1},{65,33},{97,65},{2,98}... | collective-permute-start | bytes 196616 | tf_op jit(solution)/shard_map/ppermute | solution.py:44
  141.1 8.3 %collective-permute-start.17 = (bf16[16,2048]{1,0:T(8,128)(2,1)S(1)}, bf16[16,2048]{1,0:T(8,128)(2,1)S(1)}, u32[]{:S(2)}, u32[]{:S(2)}) collective-permute-start(bf16[16,2048]{1,0:T(8,128)(2,1)S(1)} %convolution_convert_fusion.17), channel_id=1, source_target_pairs={{0,32},{32,64},{64,96},{96,0},{1,33},{33,65},{65,97},{97,1},{2,34}... | collective-permute-start | bytes 196616 | tf_op jit(solution)/shard_map/ppermute | solution.py:44
  141.1 9.0 %collective-permute-start.16 = (bf16[16,2048]{1,0:T(8,128)(2,1)S(1)}, bf16[16,2048]{1,0:T(8,128)(2,1)S(1)}, u32[]{:S(2)}, u32[]{:S(2)}) collective-permute-start(bf16[16,2048]{1,0:T(8,128)(2,1)S(1)} %convolution_convert_fusion.17), channel_id=1, source_target_pairs={{0,64},{32,96},{64,0},{96,32},{1,65},{33,97},{65,1},{97,33},{2,66}... | collective-permute-start | bytes 196616 | tf_op jit(solution)/shard_map/ppermute | solution.py:44
  150.2 10.5 %collective-permute-start.21 = (bf16[16,2048]{1,0:T(8,128)(2,1)S(1)}, bf16[16,2048]{1,0:T(8,128)(2,1)S(1)}, u32[]{:S(2)}, u32[]{:S(2)}) collective-permute-start(bf16[16,2048]{1,0:T(8,128)(2,1)S(1)} %add_convert_fusion), channel_id=1, source_target_pairs={{0,24},{8,0},{16,8},{24,16},{1,25},{9,1},{17,9},{25,17},{2,26},{10... | collective-permute-start | bytes 196616 | tf_op jit(solution)/shard_map/ppermute | solution.py:44
  154.4 7.7 %collective-permute-start.20 = (bf16[16,2048]{1,0:T(8,128)(2,1)S(1)}, bf16[16,2048]{1,0:T(8,128)(2,1)S(1)}, u32[]{:S(2)}, u32[]{:S(2)}) collective-permute-start(bf16[16,2048]{1,0:T(8,128)(2,1)S(1)} %add_convert_fusion), channel_id=1, source_target_pairs={{0,8},{8,16},{16,24},{24,0},{1,9},{9,17},{17,25},{25,1},{2,10},{10... | collective-permute-start | bytes 196616 | tf_op jit(solution)/shard_map/ppermute | solution.py:44
  154.4 7.8 %collective-permute-start.19 = (bf16[16,2048]{1,0:T(8,128)(2,1)S(1)}, bf16[16,2048]{1,0:T(8,128)(2,1)S(1)}, u32[]{:S(2)}, u32[]{:S(2)}) collective-permute-start(bf16[16,2048]{1,0:T(8,128)(2,1)S(1)} %add_convert_fusion), channel_id=1, source_target_pairs={{0,16},{8,24},{16,0},{24,8},{1,17},{9,25},{17,1},{25,9},{2,18},{10... | collective-permute-start | bytes 196616 | tf_op jit(solution)/shard_map/ppermute | solution.py:44
  157.0 45.6 %all-to-all-start = ((bf16[8,64,2048]{2,1,0:T(8,128)(2,1)}), bf16[8,64,2048]{2,1,0:T(8,128)(2,1)S(1)}, u32[]{:S(2)}, u32[]{:S(2)}) async-start(bf16[8,64,2048]{2,1,0:T(8,128)(2,1)} %dynamic-slice_dynamic-update-slice_fusion), calls=%async_computation | async-start | bytes 4194304 | tf_op jit(solution)/shard_map/all_to_all | solution.py:38
  (28 other events, 182.8 us)
Sparse Core Ops, SparseCore 0:
  97.5 125.8 reduce-scatter.1
